TPU v7x, 32 devices: a whole 2x2x4 slice. The times are simulated.
32 devices in a mesh: grid: 16 (over z, x, core), band: 2 (over y).
Axes of the slice: x: 2, y: 2, z: 4, core: 2. Of those that a mesh axis runs over, the one named last changes fastest.
Arguments:
- left_bands: float32 [2, 8, 128, 128, 128], P(None, 'band', 'grid'), may hold values from -6 to 6
- right_bands: float32 [2, 4, 128, 128, 128], P(None, 'band', 'grid'), may hold values from -6 to 6
- sphere_index: int32 [16384], replicated, may hold values from 0 to 2097151, as said below
- right_order: int32 [4], replicated, may hold values from 0 to 3, each once
Outputs:
- pair_density: float32 [2, 8, 4, 16384], P(None, 'band', None, 'grid')
Inputs may be any that keep to these rules, and one draw needn't show every extreme that they name: `sphere_index`: flat index (kz * 128 + ky) * 128 + kx; an index may repeat. In each aligned block of 1024 entries, at most 64 entries share one value of ky // 8, and some value is shared by exactly 64. `right_order`: each second band once.
All inputs are finite; a program needn't handle non-finite values.
Results may differ from a plain program's by a relative error of at most 0.00008.
Values sent between devices are 32-bit elements; how exact they have to be, the bound alone decides.
No kernel may reach another device: no remote copies, remote signals or barrier semaphores. Data moves between devices by JAX's collectives and lax.ppermute only.
A program may use at most 256 MiB of HBM per device.

v0:
```python
from functools import partial
import math

import jax
import jax.numpy as jnp
import numpy as np
from jax import lax
from jax.experimental import pallas as pl
from jax.experimental.pallas import tpu as pltpu
from jax.sharding import PartitionSpec as P


F32 = jnp.float32
BF16 = jnp.bfloat16
LANES = 128
SUB = 8
SPAN = 3


def swapped(block, axis, apart):
    count = lax.axis_size(axis)
    route = []
    for low in range(count):
        high = low | 1 << apart
        if high != low and high < count:
            route += [(low, high), (high, low)]
    return lax.ppermute(block, axis, route)


def dft_parts(length):
    counter = np.arange(length)
    angles = (counter[:, None] * counter[None, :] % length) * (2.0 * math.pi / length)
    return np.cos(angles), np.sin(angles)


def two_terms(table):
    high = np.asarray(table, BF16)
    return high, np.asarray(table - np.asarray(high, np.float32), BF16)


def rows_table(length):
    cosine, sine = dft_parts(length)
    return np.block([[cosine, sine], [-sine, cosine]]).astype(np.float32)


def lanes_table(length):
    cosine, sine = dft_parts(length)
    return np.block([[cosine, -sine], [sine, cosine]]).astype(np.float32)


def left_table(table):
    high, low = two_terms(table)
    return jnp.asarray(np.concatenate([high, low, high], axis=1))


def right_table(table):
    high, low = two_terms(table)
    return jnp.asarray(np.concatenate([high, high, low], axis=0))


def split(value):
    high = value.astype(BF16)
    return high, (value - high.astype(F32)).astype(BF16)


def dot(a, b):
    return jnp.dot(a, b, preferred_element_type=F32)


def taken(value, lanes):
    return jnp.take_along_axis(value, lanes, axis=1, mode="promise_in_bounds")


def turned(number, count):
    back = 0
    while count > 1:
        back, number, count = 2 * back + number % 2, number // 2, count // 2
    return back


def chunk_kernel(
    plan, starts_ref, left_ref, right_ref, table_y_ref, table_x_ref, picks_ref, places_ref, turns_ref,
    *rest,
):
    if plan["add"]:
        before_ref, *rest = rest
    out_ref, h_real, h_imag, f_even, f_odd, hold_ref = rest
    lefts, rights, planes = plan["lefts"], plan["rights"], plan["planes"]
    pairs = lefts * rights
    halves, tiles, stride = plan["halves"], plan["tiles"], plan["stride"]
    length, groups, rows, chunks = plan["length"], plan["groups"], plan["rows"], plan["chunks"]
    wide = tiles * SUB

    def transform_rows(z, _):
        if halves == 2:
            slot = (z % tiles) * SUB + (z // tiles) * pairs
        else:
            slot = z * SUB
        for first in range(0, pairs, 2):
            fields = []
            for pair in (first, first + 1):
                m, n = pair // lefts, pair % lefts
                lr, li = left_ref[0, n, z], left_ref[1, n, z]
                rr, ri = right_ref[0, m, z], right_ref[1, m, z]
                fields.append(jnp.concatenate([lr * rr + li * ri, lr * ri - li * rr], axis=0))
            high, low = split(jnp.concatenate(fields, axis=1))
            moved = dot(table_y_ref[...], jnp.concatenate([high, high, low], axis=0))
            for k in range(2):
                spot = pl.ds(slot + first + k, length, stride=stride)
                lanes = slice(k * LANES, (k + 1) * LANES)
                h_real[spot, :] = moved[:length, lanes]
                h_imag[spot, :] = moved[length:, lanes]
        return 0

    lax.fori_loop(0, planes, transform_rows, 0)

    def transform_lanes(group, f_ref):
        spots = [pl.ds((group * rows + y) * stride, wide) for y in range(rows)]
        real = jnp.concatenate([h_real[spot, :] for spot in spots], axis=0)
        imag = jnp.concatenate([h_imag[spot, :] for spot in spots], axis=0)
        high, low = split(jnp.concatenate([real, imag], axis=1))
        moved = dot(jnp.concatenate([high, low, high], axis=1), table_x_ref[...])
        for y in range(rows):
            f_ref[y] = moved[y * wide : (y + 1) * wide]

    upper = lax.broadcasted_iota(jnp.int32, (SUB, LANES), 0) >= SUB // 2
    late = lax.broadcasted_iota(jnp.int32, (SUB, LANES), 1) >= LANES // 2
    span = plan["span"]

    def wide_row(ref, at, *k):
        return jnp.broadcast_to(ref[k + (pl.ds(at, 1), slice(None))], (SUB, LANES))

    def box(y, tile, part):
        rows_of, lanes_of = pl.ds(tile * SUB, SUB), pl.ds(part * LANES, LANES)
        return (y, rows_of, lanes_of)

    def near(at, f_ref):
        lanes = wide_row(picks_ref, at, 0)
        start = starts_ref[at]
        apart = wide_row(picks_ref, at, 1) - start
        same = [apart == y for y in range(span)]

        def value(tile, part):
            best = taken(f_ref[box(start, tile, part)], lanes)
            for y in range(1, span):
                best = jnp.where(same[y], taken(f_ref[box(start + y, tile, part)], lanes), best)
            return best

        return value

    def far(at, f_ref):
        lanes = wide_row(picks_ref, at, 0)
        y_of = wide_row(picks_ref, at, 1)

        def value(tile, part):
            def body(y, best):
                return jnp.where(y_of == y, taken(f_ref[box(y, tile, part)], lanes), best)

            return lax.fori_loop(0, rows, body, jnp.zeros((SUB, LANES), F32))

        return value

    def picked(at, value):
        turn_r, turn_i = wide_row(turns_ref, at, 0), wide_row(turns_ref, at, 1)
        base_r, base_i = wide_row(turns_ref, at, 2), wide_row(turns_ref, at, 3)
        if halves == 2:
            base_r = jnp.where(upper, wide_row(turns_ref, at, 4), base_r)
            base_i = jnp.where(upper, wide_row(turns_ref, at, 5), base_i)
        real, imag = value(tiles - 1, 0), value(tiles - 1, 1)
        for tile in reversed(range(tiles - 1)):
            real, imag = (
                real * turn_r - imag * turn_i + value(tile, 0),
                real * turn_i + imag * turn_r + value(tile, 1),
            )
        real, imag = real * base_r - imag * base_i, real * base_i + imag * base_r
        if pairs == SUB:
            found = [real, imag]
        else:
            if halves == 2:
                real = real + pltpu.roll(real, SUB // 2, 0)
                imag = imag + pltpu.roll(imag, SUB // 2, 0)
            else:
                imag = pltpu.roll(imag, SUB // 2, 0)
            found = [jnp.where(upper, imag, real)]
        if plan["add"]:
            found = [one + before_ref[at, part] for part, one in enumerate(found)]
        return found

    def moved_back(group, found):
        result = []
        for chunk in range(chunks):
            place = wide_row(places_ref, group * chunks + chunk)
            lanes, source = place % LANES, place // LANES
            parts = []
            for part in range(len(found[0])):
                best = taken(found[0][part], lanes)
                for other in range(1, chunks):
                    best = jnp.where(source == other, taken(found[other][part], lanes), best)
                parts.append(best)
            result.append(parts)
        return result

    def group_sums(group, f_ref, look):
        found = []
        for chunk in range(chunks):
            at = group * chunks + chunk
            found.append(picked(at, look(at, f_ref)))
        if not plan["last"]:
            for chunk in range(chunks):
                for part, value in enumerate(found[chunk]):
                    out_ref[group * chunks + chunk, part] = value
            return found
        return moved_back(group, found)

    def put_couple(a, firsts, seconds):
        place = pl.ds(pl.multiple_of(a * LANES, LANES), LANES)
        for chunk in range(chunks):
            for part, (one, two) in enumerate(zip(firsts[chunk], seconds[chunk])):
                low, high = turned(2 * chunk, groups), turned(2 * chunk + 1, groups)
                out_ref[low, part, :, place] = jnp.where(late, pltpu.roll(two, LANES // 2, 1), one)
                out_ref[high, part, :, place] = jnp.where(late, two, pltpu.roll(one, LANES // 2, 1))

    def put_single(group, found):
        for chunk in range(chunks):
            for part, value in enumerate(found[chunk]):
                out_ref[group * chunks + chunk, part] = value

    @pl.when(starts_ref[groups * chunks] == 1)
    def _():
        if groups % 2:

            def single(group, _):
                transform_lanes(group, f_even)
                found = group_sums(group, f_even, near)
                if plan["last"]:
                    put_single(group, found)
                return 0

            lax.fori_loop(0, groups, single, 0)
            return
        transform_lanes(0, f_even)

        def couple(a, _):
            transform_lanes(2 * a + 1, f_odd)
            firsts = group_sums(2 * a, f_even, near)
            transform_lanes(jnp.minimum(2 * a + 2, groups - 1), f_even)
            seconds = group_sums(2 * a + 1, f_odd, near)
            if plan["last"]:
                if plan["woven"]:
                    put_couple(a, firsts, seconds)
                else:
                    put_single(2 * a, firsts)
                    put_single(2 * a + 1, seconds)
            return 0

        lax.fori_loop(0, groups // 2, couple, 0)

    @pl.when(starts_ref[groups * chunks] == 0)
    def _():
        def compute(group):
            transform_lanes(group, f_even)

            def body(chunk, _):
                at = group * chunks + chunk
                for part, value in enumerate(picked(at, far(at, f_even))):
                    hold_ref[chunk, part] = value
                return 0

            lax.fori_loop(0, chunks, body, 0)
            count = 2 if pairs == SUB else 1
            found = [[hold_ref[chunk, part] for part in range(count)] for chunk in range(chunks)]
            return moved_back(group, found) if plan["last"] else found

        if plan["last"] and plan["woven"]:

            def couple(a, _):
                firsts = compute(2 * a)
                put_couple(a, firsts, compute(2 * a + 1))
                return 0

            lax.fori_loop(0, groups // 2, couple, 0)
        else:

            def single(group, _):
                put_single(group, compute(group))
                return 0

            lax.fori_loop(0, groups, single, 0)


def is_woven(sizes):
    groups, slots = sizes
    return 2 * slots == LANES and groups % 2 == 0


def chunk_sums(left, right, tables, lists, turns, before, last, sizes):
    lefts, rights = left.shape[1], right.shape[1]
    planes, length = left.shape[2], left.shape[3]
    groups, slots = sizes
    pairs = lefts * rights
    halves = 2 if pairs < SUB and planes % 2 == 0 else 1
    tiles = planes // halves
    wide = tiles * SUB
    stride = wide if tiles % 2 else wide + SUB
    parts = 2 * pairs // SUB
    chunks = groups * slots // LANES
    woven = is_woven(sizes)
    plan = dict(
        lefts=lefts, rights=rights, planes=planes, halves=halves, tiles=tiles, stride=stride,
        length=length, groups=groups, rows=length // groups, chunks=chunks, woven=woven,
        add=before is not None, last=last, span=min(SPAN, length // groups),
    )
    if woven and last:
        shape = (groups, parts, SUB, groups * slots)
    else:
        shape = (groups * chunks, parts, SUB, LANES)
    starts, picks, places = lists
    operands = [starts, left, right, *tables, picks, places, turns]
    if before is not None:
        operands.append(before)
    field = pltpu.VMEM((length * stride, LANES), F32)
    group = pltpu.VMEM((length // groups, wide, 2 * LANES), F32)
    flops = 2 * 3 * 2 * pairs * planes * length * (2 * length) * (2 * length)
    return pl.pallas_call(
        partial(chunk_kernel, plan),
        out_shape=jax.ShapeDtypeStruct(shape, F32),
        in_specs=[pl.BlockSpec(memory_space=pltpu.SMEM)]
        + [pl.BlockSpec(memory_space=pltpu.VMEM)] * (len(operands) - 1),
        scratch_shapes=[field, field, group, group, pltpu.VMEM((chunks, parts, SUB, LANES), F32)],
        compiler_params=pltpu.CompilerParams(vmem_limit_bytes=58 * 1024 * 1024),
        cost_estimate=pl.CostEstimate(flops=flops, bytes_accessed=4 * left.size, transcendentals=0),
    )(*operands)


def to_owner(sums, sizes):
    groups, slots = sizes
    if is_woven(sizes):
        return sums
    parts = sums.shape[1]
    shaped = sums.reshape(groups, -1, parts, SUB, LANES)
    shaped = jnp.moveaxis(shaped, 1, 3).reshape(groups, parts, SUB, groups, slots)
    shaped = jnp.transpose(shaped, (3, 1, 2, 0, 4)).reshape(groups, parts, SUB, groups * slots)
    return shaped[np.array([turned(owner, groups) for owner in range(groups)])]


def halved_sum(sums, axis):
    count = sums.shape[0]
    me = lax.axis_index(axis)
    apart = 1
    while sums.shape[0] > 1:
        half = sums.shape[0] // 2
        side = me // apart % 2
        sent = lax.dynamic_slice_in_dim(sums, (1 - side) * half, half, 0)
        kept = lax.dynamic_slice_in_dim(sums, side * half, half, 0)
        route = [(device, device ^ apart) for device in range(count)]
        sums = kept + lax.ppermute(sent, axis, route)
        apart *= 2
    return sums


def order_kernel(subs, key_ref, sorted_ref, place_ref):
    size, width = key_ref.shape[1], key_ref.shape[0]
    total = size * subs
    row = lax.broadcasted_iota(jnp.int32, (size, width), 0)
    lane = lax.broadcasted_iota(jnp.int32, (size, width), 1)
    spot = lane % subs * size + row

    def sort(value):
        span = 2
        while span <= total:
            apart = span // 2
            rising = spot & span == 0
            while apart > 0:
                first = spot & apart == 0
                if apart < size:
                    axis, shift, full = 0, apart, size
                else:
                    axis, shift, full = 1, apart // size, width
                other = jnp.where(
                    first, pltpu.roll(value, full - shift, axis), pltpu.roll(value, shift, axis)
                )
                small, large = jnp.minimum(value, other), jnp.maximum(value, other)
                value = jnp.where(first == rising, small, large)
                apart //= 2
            span *= 2
        return value

    value = sort(key_ref[...].T)
    sorted_ref[...] = value.T
    back = sort(value % total * total + spot)
    place_ref[...] = (back % total).T


def ordered(key, per_block):
    shape = (key.size // LANES, LANES)
    like = jax.ShapeDtypeStruct(shape, jnp.int32)
    return pl.pallas_call(
        partial(order_kernel, per_block // LANES), out_shape=[like, like]
    )(key.reshape(shape))


def finish_kernel(scale, count, own_rights, order_ref, place_ref, own_ref, *rest):
    others, out_ref, hold_ref = rest[:count], rest[count], rest[count + 1]
    length = out_ref.shape[-1]
    lefts = out_ref.shape[1]
    half = SUB // 2

    def total(ref, part):
        value = ref[0, part]
        for source in range(1, ref.shape[0]):
            value = value + ref[source, part]
        return value * scale

    blocks = [[total(own_ref, part) for part in range(own_ref.shape[1])]]
    if len(blocks[0]) == 2:
        real, imag = blocks[0]
        for m in range(own_rights):
            rows = slice(m * lefts, (m + 1) * lefts)
            hold_ref[m] = jnp.concatenate([real[rows], imag[rows]], axis=0)
    for k, ref in enumerate(others):
        hold_ref[own_rights + k] = total(ref, 0)
    pieces = length // LANES
    for j in range(out_ref.shape[2]):
        block = hold_ref[order_ref[j]]
        for piece in range(pieces):
            lanes = slice(piece * LANES, (piece + 1) * LANES)
            place = jnp.broadcast_to(place_ref[:, lanes], (SUB, LANES))
            inner = place % LANES
            outer = place // LANES
            best = taken(block[:, :LANES], inner)
            for source in range(1, pieces):
                more = taken(block[:, source * LANES : (source + 1) * LANES], inner)
                best = jnp.where(outer == source, more, best)
            for n in range(lefts):
                out_ref[0, n, j : j + 1, lanes] = best[n : n + 1]
                out_ref[1, n, j : j + 1, lanes] = best[half + n : half + n + 1]


def finished(own, others, order, place, shape, scale, own_rights):
    count = own_rights + len(others)
    return pl.pallas_call(
        partial(finish_kernel, scale, len(others), own_rights),
        out_shape=jax.ShapeDtypeStruct(shape, F32),
        in_specs=[pl.BlockSpec(memory_space=pltpu.SMEM)]
        + [pl.BlockSpec(memory_space=pltpu.VMEM)] * (2 + len(others)),
        scratch_shapes=[pltpu.VMEM((count, SUB, shape[-1]), F32)],
        compiler_params=pltpu.CompilerParams(vmem_limit_bytes=58 * 1024 * 1024),
    )(order, place, own, *others)


def local(left_bands, right_bands, sphere_index, right_order):
    lefts, own_rights, planes = left_bands.shape[1], right_bands.shape[1], left_bands.shape[2]
    length, width = left_bands.shape[3], left_bands.shape[4]
    groups = lax.axis_size("grid")
    me = lax.axis_index("grid")
    per_block = sphere_index.shape[0] // groups
    slots = per_block // groups
    rows = length // groups
    sizes = (groups, slots)
    cuts = [(0, planes)] if planes < 4 else [(0, planes // 2), (planes // 2, planes)]
    routes = [(0, 0, planes)] + [(1, low, high) for low, high in cuts]
    sent = []
    for m, low, high in routes:
        sent.append(swapped(right_bands[:, m : m + 1, low:high], "band", 0))

    wave_z = sphere_index // (length * width)
    wave_y = sphere_index // width % length
    wave_x = sphere_index % width
    spot = jnp.arange(sphere_index.shape[0], dtype=jnp.int32) % per_block
    key = ((wave_y * length + wave_z) * width + wave_x) * per_block + spot
    key, place = ordered(key, per_block)
    place = lax.dynamic_slice_in_dim(place.reshape(groups, per_block), me, 1, 0)
    key = jnp.transpose(key.reshape(groups, groups, slots), (1, 0, 2)) // per_block
    spot = jnp.arange(groups * slots, dtype=jnp.int32).reshape(groups, slots)
    key, places = ordered((key % (rows * length * width)) * (groups * slots) + spot, groups * slots)
    key = key // (groups * slots)
    row_of = key // (width * length)
    picks = jnp.stack([key % width, row_of])
    starts = jnp.clip(row_of[:, 0], 0, rows - min(SPAN, rows))
    near = jnp.all(row_of[:, -1] - starts < SPAN).astype(jnp.int32)
    lists = (jnp.concatenate([starts, near[None]]), picks, places)
    plane_wave = key // width % length

    def turn(z):
        angle = (plane_wave * z % length).astype(F32) * (2.0 * math.pi / length)
        return [jnp.cos(angle), -jnp.sin(angle)]

    tables = (left_table(rows_table(length)), right_table(lanes_table(width)))

    def sums(right, low, high, before, last):
        start = me * planes + low
        turns = jnp.stack(turn(1) + turn(start) + turn(start + (high - low) // 2))
        return chunk_sums(
            left_bands[:, :, low:high], right, tables, lists, turns, before, last, sizes
        )

    def owned(value):
        return halved_sum(to_owner(value, sizes), "grid")

    own_sums = sums(right_bands, 0, planes, None, True)
    right, _ = lax.optimization_barrier((sent[0], own_sums))
    first_sums = sums(right, 0, planes, None, True)
    last_sums, ahead = None, first_sums
    for right, (_, low, high) in zip(sent[1:], routes[1:]):
        right, _ = lax.optimization_barrier((right, ahead))
        last_sums = ahead = sums(right, low, high, last_sums, high == planes)
    own, first, second = owned(own_sums), owned(first_sums), owned(last_sums)
    order = (right_order - lax.axis_index("band") * own_rights) % right_order.shape[0]
    shape = (2, lefts, right_order.shape[0], per_block)
    scale = 1.0 / (length * length * width) ** 0.5
    return finished(own, [first, second], order, place, shape, scale, own_rights)


def solution(mesh):
    placed = (P(None, "band", "grid", None, None), P(None, "band", "grid", None, None), P(), P())
    return jax.shard_map(
        local, mesh=mesh, in_specs=placed, out_specs=P(None, "band", None, "grid"), check_vma=False
    )
```

profile of v0, /device:TPU:0, one launch (start us, length us, event | category | flops | bytes accessed | tf_op | source)
XLA Modules:
  0.0 159.3 jit_solution(3904349513415934652)
XLA Ops:
  0.0 1.6 %fusion.13.key_ref = s32[128,128]{1,0:T(8,128)} fusion(s32[16384]{0:T(1024)} %param.8), kind=kLoop, calls=%fused_computation.72 | loop fusion | flops 851968 | bytes 131072 | tf_op jit(solution)/shard_map/reshape | solution.py:399
  1.6 5.4 %shard_map.64 = (s32[128,128]{1,0:T(8,128)}, s32[128,128]{1,0:T(8,128)}) custom-call(s32[128,128]{1,0:T(8,128)} %fusion.13.key_ref), custom_call_target="tpu_custom_call" | custom-call | tf_op jit(solution)/shard_map/pallas_call | solution.py:397
  8.8 5.4 %shard_map.65 = (s32[128,128]{1,0:T(8,128)}, s32[128,128]{1,0:T(8,128)}) custom-call(s32[128,128]{1,0:T(8,128)} %reshape.28.key_ref), custom_call_target="tpu_custom_call" | custom-call | tf_op jit(solution)/shard_map/pallas_call | solution.py:397
  26.8 22.2 %shard_map.66 = f32[16,2,8,1024]{3,2,1,0:T(8,128)} custom-call(s32[129]{0:T(256)} %pad_add_fusion.1.starts_ref, f32[2,4,8,128,128]{4,3,2,1,0:T(8,128)} %left_ref.3, f32[2,2,8,128,128]{4,3,2,1,0:T(8,128)} %right_ref.1, bf16[256,768]{1,0:T(8,128)(2,1)} %constant.299.clone.table_y_ref, bf16[768,256]{1,0:T(8,128)(2,1)} %constant.300.clone.table_x_ref, ...), custom_call_target="tpu_custom_call" | custom-call | flops 6442450944 | bytes 4194304 | tf_op jit(solution)/shard_map/pallas_call | solution.py:324
  51.8 2.5 %collective-permute-start.10 = (f32[2,1,4,128,128]{4,3,2,1,0:T(8,128)}, f32[2,1,4,128,128]{4,3,2,1,0:T(8,128)}, u32[]{:S(2)}, u32[]{:S(2)}) collective-permute-start(f32[2,1,4,128,128]{4,3,2,1,0:T(8,128)} %get-tuple-element.23), channel_id=1, source_target_pairs={{0,1},{1,0},{2,3},{3,2},{4,5},{5,4},{6,7},{7,6},{8,9},{9,8},{10,11... | collective-permute-start | bytes 1572872 | tf_op jit(solution)/shard_map/ppermute | solution.py:27
  54.5 2.1 %collective-permute-start.4 = (f32[2,1,8,128,128]{4,3,2,1,0:T(8,128)S(1)}, f32[2,1,8,128,128]{4,3,2,1,0:T(8,128)}, u32[]{:S(2)}, u32[]{:S(2)}) collective-permute-start(f32[2,1,8,128,128]{4,3,2,1,0:T(8,128)S(1)} %slice.23), channel_id=1, source_target_pairs={{0,1},{1,0},{2,3},{3,2},{4,5},{5,4},{6,7},{7,6},{8,9},{9,8},{10,11... | collective-permute-start | bytes 3145736 | tf_op jit(solution)/shard_map/ppermute | solution.py:27
  58.3 4.7 %fusion.50 = (f32[2,4,4,128,128]{4,3,2,1,0:T(8,128)}, f32[2,4,4,128,128]{4,3,2,1,0:T(8,128)}) fusion(f32[2,4,8,128,128]{4,3,2,1,0:T(8,128)} %left_ref.3), kind=kLoop, calls=%fused_computation.160 | loop fusion | bytes 8388608 | tf_op jit(solution)/shard_map/slice | solution.py:494
  63.0 1.7 %collective-permute-done.1 = f32[4,2,8,1024]{3,2,1,0:T(8,128)S(1)} collective-permute-done((f32[4,2,8,1024]{3,2,1,0:T(8,128)S(1)}, f32[4,2,8,1024]{3,2,1,0:T(8,128)S(1)}, u32[]{:S(2)}, u32[]{:S(2)}) %collective-permute-start.1) | collective-permute-done | bytes 262176 | tf_op jit(solution)/shard_map/ppermute | solution.py:356
  64.7 1.6 %collective-permute-start.2 = (f32[2,2,8,1024]{3,2,1,0:T(8,128)S(1)}, f32[2,2,8,1024]{3,2,1,0:T(8,128)S(1)}, u32[]{:S(2)}, u32[]{:S(2)}) collective-permute-start(f32[2,2,8,1024]{3,2,1,0:T(8,128)S(1)} %constant_dynamic-slice_fusion.9), channel_id=1, source_target_pairs={{0,8},{2,10},{4,12},{6,14},{8,0},{10,2},{12,4},{14,6},{16,24},{18,... | collective-permute-start | bytes 393224 | tf_op jit(solution)/shard_map/ppermute | solution.py:356
  66.9 2.9 %collective-permute-done.2 = f32[2,2,8,1024]{3,2,1,0:T(8,128)S(1)} collective-permute-done((f32[2,2,8,1024]{3,2,1,0:T(8,128)S(1)}, f32[2,2,8,1024]{3,2,1,0:T(8,128)S(1)}, u32[]{:S(2)}, u32[]{:S(2)}) %collective-permute-start.2) | collective-permute-done | bytes 131104 | tf_op jit(solution)/shard_map/ppermute | solution.py:356
  69.8 2.6 %collective-permute-start.3 = (f32[1,2,8,1024]{3,2,1,0:T(8,128)S(1)}, f32[1,2,8,1024]{3,2,1,0:T(8,128)S(1)}, u32[]{:S(2)}, u32[]{:S(2)}) collective-permute-start(f32[1,2,8,1024]{3,2,1,0:T(8,128)S(1)} %constant_dynamic-slice_fusion.8), channel_id=1, source_target_pairs={{0,16},{2,18},{4,20},{6,22},{8,24},{10,26},{12,28},{14,30},{16,0},... | collective-permute-start | bytes 196616 | tf_op jit(solution)/shard_map/ppermute | solution.py:356
  73.0 2.0 %collective-permute-done.3 = f32[1,2,8,1024]{3,2,1,0:T(8,128)S(1)} collective-permute-done((f32[1,2,8,1024]{3,2,1,0:T(8,128)S(1)}, f32[1,2,8,1024]{3,2,1,0:T(8,128)S(1)}, u32[]{:S(2)}, u32[]{:S(2)}) %collective-permute-start.3) | collective-permute-done | bytes 65568 | tf_op jit(solution)/shard_map/ppermute | solution.py:356
  75.7 25.3 %collective-permute-done.4.right_ref = f32[2,1,8,128,128]{4,3,2,1,0:T(8,128)} collective-permute-done((f32[2,1,8,128,128]{4,3,2,1,0:T(8,128)S(1)}, f32[2,1,8,128,128]{4,3,2,1,0:T(8,128)}, u32[]{:S(2)}, u32[]{:S(2)}) %collective-permute-start.4) | collective-permute-done | bytes 1048608 | tf_op jit(solution)/shard_map/ppermute | solution.py:27
  101.0 15.2 %shard_map.67 = f32[16,1,8,1024]{3,2,1,0:T(8,128)} custom-call(s32[129]{0:T(256)} %pad_add_fusion.1.starts_ref, f32[2,4,8,128,128]{4,3,2,1,0:T(8,128)} %left_ref.3, f32[2,1,8,128,128]{4,3,2,1,0:T(8,128)} %collective-permute-done.4.right_ref, bf16[256,768]{1,0:T(8,128)(2,1)} %constant.299.clone.table_y_ref, bf16[768,256]{1,0:T(8,128)(2,1)} %constant.300.clone.table_x_ref, ...), custom_call_target="tpu_custom_call" | custom-call | flops 3221225472 | bytes 4194304 | tf_op jit(solution)/shard_map/pallas_call | solution.py:324
  117.2 8.7 %shard_map.68.rest_0_ = f32[128,1,8,128]{3,2,1,0:T(8,128)} custom-call(s32[129]{0:T(256)} %pad_add_fusion.1.starts_ref, f32[2,4,4,128,128]{4,3,2,1,0:T(8,128)} %get-tuple-element.21.left_ref, f32[2,1,4,128,128]{4,3,2,1,0:T(8,128)} %collective-permute-done.10.right_ref, bf16[256,768]{1,0:T(8,128)(2,1)} %constant.299.clone.table_y_ref, ...), custom_call_target="tpu_custom_call" | custom-call | flops 1610612736 | bytes 2097152 | tf_op jit(solution)/shard_map/pallas_call | solution.py:324
  125.9 11.1 %shard_map.69 = f32[16,1,8,1024]{3,2,1,0:T(8,128)} custom-call(s32[129]{0:T(256)} %pad_add_fusion.1.starts_ref, f32[2,4,4,128,128]{4,3,2,1,0:T(8,128)} %get-tuple-element.22.left_ref, f32[2,1,4,128,128]{4,3,2,1,0:T(8,128)} %collective-permute-done.9.right_ref, bf16[256,768]{1,0:T(8,128)(2,1)} %constant.299.clone.table_y_ref, ...), custom_call_target="tpu_custom_call" | custom-call | flops 1610612736 | bytes 2097152 | tf_op jit(solution)/shard_map/pallas_call | solution.py:324
  138.6 1.7 %collective-permute-start.6 = (f32[4,1,8,1024]{3,2,1,0:T(8,128)S(1)}, f32[4,1,8,1024]{3,2,1,0:T(8,128)S(1)}, u32[]{:S(2)}, u32[]{:S(2)}) collective-permute-start(f32[4,1,8,1024]{3,2,1,0:T(8,128)S(1)} %constant_dynamic-slice_fusion.6), channel_id=1, source_target_pairs={{0,4},{2,6},{4,0},{6,2},{8,12},{10,14},{12,8},{14,10},{16,20},{18,... | collective-permute-start | bytes 393224 | tf_op jit(solution)/shard_map/ppermute | solution.py:356
  142.5 2.0 %collective-permute-done.6 = f32[4,1,8,1024]{3,2,1,0:T(8,128)S(1)} collective-permute-done((f32[4,1,8,1024]{3,2,1,0:T(8,128)S(1)}, f32[4,1,8,1024]{3,2,1,0:T(8,128)S(1)}, u32[]{:S(2)}, u32[]{:S(2)}) %collective-permute-start.6) | collective-permute-done | bytes 131104 | tf_op jit(solution)/shard_map/ppermute | solution.py:356
  144.5 1.8 %collective-permute-start.7 = (f32[2,1,8,1024]{3,2,1,0:T(8,128)S(1)}, f32[2,1,8,1024]{3,2,1,0:T(8,128)S(1)}, u32[]{:S(2)}, u32[]{:S(2)}) collective-permute-start(f32[2,1,8,1024]{3,2,1,0:T(8,128)S(1)} %constant_dynamic-slice_fusion.5), channel_id=1, source_target_pairs={{0,8},{2,10},{4,12},{6,14},{8,0},{10,2},{12,4},{14,6},{16,24},{18,... | collective-permute-start | bytes 196616 | tf_op jit(solution)/shard_map/ppermute | solution.py:356
  147.0 1.8 %collective-permute-start.13 = (f32[2,1,8,1024]{3,2,1,0:T(8,128)S(1)}, f32[2,1,8,1024]{3,2,1,0:T(8,128)S(1)}, u32[]{:S(2)}, u32[]{:S(2)}) collective-permute-start(f32[2,1,8,1024]{3,2,1,0:T(8,128)S(1)} %constant_dynamic-slice_fusion.1), channel_id=1, source_target_pairs={{0,8},{2,10},{4,12},{6,14},{8,0},{10,2},{12,4},{14,6},{16,24},{18,... | collective-permute-start | bytes 196616 | tf_op jit(solution)/shard_map/ppermute | solution.py:356
  148.8 2.9 %collective-permute-start.8 = (f32[1,1,8,1024]{3,2,1,0:T(8,128)S(1)}, f32[1,1,8,1024]{3,2,1,0:T(8,128)S(1)}, u32[]{:S(2)}, u32[]{:S(2)}) collective-permute-start(f32[1,1,8,1024]{3,2,1,0:T(8,128)S(1)} %constant_dynamic-slice_fusion.4), channel_id=1, source_target_pairs={{0,16},{2,18},{4,20},{6,22},{8,24},{10,26},{12,28},{14,30},{16,0},... | collective-permute-start | bytes 98312 | tf_op jit(solution)/shard_map/ppermute | solution.py:356
  151.8 2.4 %collective-permute-start.14 = (f32[1,1,8,1024]{3,2,1,0:T(8,128)S(1)}, f32[1,1,8,1024]{3,2,1,0:T(8,128)S(1)}, u32[]{:S(2)}, u32[]{:S(2)}) collective-permute-start(f32[1,1,8,1024]{3,2,1,0:T(8,128)S(1)} %constant_dynamic-slice_fusion), channel_id=1, source_target_pairs={{0,16},{2,18},{4,20},{6,22},{8,24},{10,26},{12,28},{14,30},{16,0},... | collective-permute-start | bytes 98312 | tf_op jit(solution)/shard_map/ppermute | solution.py:356
  154.8 1.8 %collective-permute-done.14 = f32[1,1,8,1024]{3,2,1,0:T(8,128)S(1)} collective-permute-done((f32[1,1,8,1024]{3,2,1,0:T(8,128)S(1)}, f32[1,1,8,1024]{3,2,1,0:T(8,128)S(1)}, u32[]{:S(2)}, u32[]{:S(2)}) %collective-permute-start.14) | collective-permute-done | bytes 32800 | tf_op jit(solution)/shard_map/ppermute | solution.py:356
  157.3 2.0 %shard_map.70 = f32[2,4,4,1024]{3,2,1,0:T(4,128)} custom-call(s32[4]{0:T(128)} %and_select_fusion.order_ref, s32[1,1024]{1,0:T(1,128)} %constant_dynamic-slice_fusion.12.place_ref, f32[1,2,8,1024]{3,2,1,0:T(8,128)} %dynamic-slice_add_fusion.9.own_ref, f32[1,1,8,1024]{3,2,1,0:T(8,128)} %dynamic-slice_add_fusion.11.rest_0_, ...), custom_call_target="tpu_custom_call" | custom-call | tf_op jit(solution)/shard_map/pallas_call | solution.py:441
  (81 shorter events, 26.7 us)
Async XLA Ops:
  14.2 10.0 %copy-start = (s32[128,128]{1,0:T(8,128)S(1)}, s32[128,128]{1,0:T(8,128)}, u32[]{:S(2)}) copy-start(s32[128,128]{1,0:T(8,128)} %get-tuple-element.14) | copy-start | bytes 196612
  26.1 0.8 copy-start.2
  26.1 23.0 %copy-start.4 = (f32[6,128,128]{2,1,0:T(8,128)}, f32[6,128,128]{2,1,0:T(8,128)S(1)}, u32[]{:S(2)}) copy-start(f32[6,128,128]{2,1,0:T(8,128)S(1)} %get-tuple-element.25.turns_ref) | copy-start | bytes 1179652
  26.1 23.0 %copy-start.6 = (f32[6,128,128]{2,1,0:T(8,128)}, f32[6,128,128]{2,1,0:T(8,128)S(1)}, u32[]{:S(2)}) copy-start(f32[6,128,128]{2,1,0:T(8,128)S(1)} %get-tuple-element.27.turns_ref) | copy-start | bytes 1179652
  26.8 23.9 %copy-start.1 = (f32[2,2,8,128,128]{4,3,2,1,0:T(8,128)S(1)}, f32[2,2,8,128,128]{4,3,2,1,0:T(8,128)}, u32[]{:S(2)}) copy-start(f32[2,2,8,128,128]{4,3,2,1,0:T(8,128)} %right_ref.1) | copy-start | bytes 6291460
  50.2 6.3 %copy-start.7 = (s32[128,128]{1,0:T(8,128)S(1)}, s32[128,128]{1,0:T(8,128)}, u32[]{:S(2)}) copy-start(s32[128,128]{1,0:T(8,128)} %get-tuple-element.12) | copy-start | bytes 196612
  50.2 6.4 %copy-start.3 = (f32[16,2,8,1024]{3,2,1,0:T(8,128)S(1)}, f32[16,2,8,1024]{3,2,1,0:T(8,128)}, u32[]{:S(2)}) copy-start(f32[16,2,8,1024]{3,2,1,0:T(8,128)} %shard_map.66) | copy-start | bytes 3145732
  50.2 6.4 %collective-permute-start = (f32[8,2,8,1024]{3,2,1,0:T(8,128)S(1)}, f32[8,2,8,1024]{3,2,1,0:T(8,128)S(1)}, u32[]{:S(2)}, u32[]{:S(2)}) collective-permute-start(f32[8,2,8,1024]{3,2,1,0:T(8,128)S(1)} %constant_dynamic-slice_fusion.11), channel_id=1, source_target_pairs={{0,2},{2,0},{4,6},{6,4},{8,10},{10,8},{12,14},{14,12},{16,18},{18,... | collective-permute-start | bytes 1572872 | tf_op jit(solution)/shard_map/ppermute | solution.py:356
  51.8 64.3 %collective-permute-start.10 = (f32[2,1,4,128,128]{4,3,2,1,0:T(8,128)}, f32[2,1,4,128,128]{4,3,2,1,0:T(8,128)}, u32[]{:S(2)}, u32[]{:S(2)}) collective-permute-start(f32[2,1,4,128,128]{4,3,2,1,0:T(8,128)} %get-tuple-element.23), channel_id=1, source_target_pairs={{0,1},{1,0},{2,3},{3,2},{4,5},{5,4},{6,7},{7,6},{8,9},{9,8},{10,11... | collective-permute-start | bytes 1572872 | tf_op jit(solution)/shard_map/ppermute | solution.py:27
  54.4 71.5 %collective-permute-start.9 = (f32[2,1,4,128,128]{4,3,2,1,0:T(8,128)}, f32[2,1,4,128,128]{4,3,2,1,0:T(8,128)}, u32[]{:S(2)}, u32[]{:S(2)}) collective-permute-start(f32[2,1,4,128,128]{4,3,2,1,0:T(8,128)} %get-tuple-element.24), channel_id=1, source_target_pairs={{0,1},{1,0},{2,3},{3,2},{4,5},{5,4},{6,7},{7,6},{8,9},{9,8},{10,11... | collective-permute-start | bytes 1572872 | tf_op jit(solution)/shard_map/ppermute | solution.py:27
  54.5 46.5 %collective-permute-start.4 = (f32[2,1,8,128,128]{4,3,2,1,0:T(8,128)S(1)}, f32[2,1,8,128,128]{4,3,2,1,0:T(8,128)}, u32[]{:S(2)}, u32[]{:S(2)}) collective-permute-start(f32[2,1,8,128,128]{4,3,2,1,0:T(8,128)S(1)} %slice.23), channel_id=1, source_target_pairs={{0,1},{1,0},{2,3},{3,2},{4,5},{5,4},{6,7},{7,6},{8,9},{9,8},{10,11... | collective-permute-start | bytes 3145736 | tf_op jit(solution)/shard_map/ppermute | solution.py:27
  56.7 9.6 %copy-start.8 = (s32[4]{0:T(128)S(1)}, s32[4]{0:T(128)}, u32[]{:S(2)}) copy-start(s32[4]{0:T(128)} %param.9) | copy-start | bytes 52
  56.7 7.9 %collective-permute-start.1 = (f32[4,2,8,1024]{3,2,1,0:T(8,128)S(1)}, f32[4,2,8,1024]{3,2,1,0:T(8,128)S(1)}, u32[]{:S(2)}, u32[]{:S(2)}) collective-permute-start(f32[4,2,8,1024]{3,2,1,0:T(8,128)S(1)} %constant_dynamic-slice_fusion.10), channel_id=1, source_target_pairs={{0,4},{2,6},{4,0},{6,2},{8,12},{10,14},{12,8},{14,10},{16,20},{18,... | collective-permute-start | bytes 786440 | tf_op jit(solution)/shard_map/ppermute | solution.py:356
  64.7 5.0 %collective-permute-start.2 = (f32[2,2,8,1024]{3,2,1,0:T(8,128)S(1)}, f32[2,2,8,1024]{3,2,1,0:T(8,128)S(1)}, u32[]{:S(2)}, u32[]{:S(2)}) collective-permute-start(f32[2,2,8,1024]{3,2,1,0:T(8,128)S(1)} %constant_dynamic-slice_fusion.9), channel_id=1, source_target_pairs={{0,8},{2,10},{4,12},{6,14},{8,0},{10,2},{12,4},{14,6},{16,24},{18,... | collective-permute-start | bytes 393224 | tf_op jit(solution)/shard_map/ppermute | solution.py:356
  69.8 5.2 %collective-permute-start.3 = (f32[1,2,8,1024]{3,2,1,0:T(8,128)S(1)}, f32[1,2,8,1024]{3,2,1,0:T(8,128)S(1)}, u32[]{:S(2)}, u32[]{:S(2)}) collective-permute-start(f32[1,2,8,1024]{3,2,1,0:T(8,128)S(1)} %constant_dynamic-slice_fusion.8), channel_id=1, source_target_pairs={{0,16},{2,18},{4,20},{6,22},{8,24},{10,26},{12,28},{14,30},{16,0},... | collective-permute-start | bytes 196616 | tf_op jit(solution)/shard_map/ppermute | solution.py:356
  117.1 21.4 %collective-permute-start.5 = (f32[8,1,8,1024]{3,2,1,0:T(8,128)S(1)}, f32[8,1,8,1024]{3,2,1,0:T(8,128)S(1)}, u32[]{:S(2)}, u32[]{:S(2)}) collective-permute-start(f32[8,1,8,1024]{3,2,1,0:T(8,128)S(1)} %constant_dynamic-slice_fusion.7), channel_id=1, source_target_pairs={{0,2},{2,0},{4,6},{6,4},{8,10},{10,8},{12,14},{14,12},{16,18},{18,... | collective-permute-start | bytes 786440 | tf_op jit(solution)/shard_map/ppermute | solution.py:356
  125.9 12.7 %copy-start.5 = (f32[16,1,8,1024]{3,2,1,0:T(8,128)S(1)}, f32[16,1,8,1024]{3,2,1,0:T(8,128)}, u32[]{:S(2)}) copy-start(f32[16,1,8,1024]{3,2,1,0:T(8,128)} %shard_map.67) | copy-start | bytes 1572868
  138.0 2.4 %collective-permute-start.11 = (f32[8,1,8,1024]{3,2,1,0:T(8,128)S(1)}, f32[8,1,8,1024]{3,2,1,0:T(8,128)S(1)}, u32[]{:S(2)}, u32[]{:S(2)}) collective-permute-start(f32[8,1,8,1024]{3,2,1,0:T(8,128)S(1)} %constant_dynamic-slice_fusion.3), channel_id=1, source_target_pairs={{0,2},{2,0},{4,6},{6,4},{8,10},{10,8},{12,14},{14,12},{16,18},{18,... | collective-permute-start | bytes 786440 | tf_op jit(solution)/shard_map/ppermute | solution.py:356
  138.6 5.8 %collective-permute-start.6 = (f32[4,1,8,1024]{3,2,1,0:T(8,128)S(1)}, f32[4,1,8,1024]{3,2,1,0:T(8,128)S(1)}, u32[]{:S(2)}, u32[]{:S(2)}) collective-permute-start(f32[4,1,8,1024]{3,2,1,0:T(8,128)S(1)} %constant_dynamic-slice_fusion.6), channel_id=1, source_target_pairs={{0,4},{2,6},{4,0},{6,2},{8,12},{10,14},{12,8},{14,10},{16,20},{18,... | collective-permute-start | bytes 393224 | tf_op jit(solution)/shard_map/ppermute | solution.py:356
  141.4 5.6 %collective-permute-start.12 = (f32[4,1,8,1024]{3,2,1,0:T(8,128)S(1)}, f32[4,1,8,1024]{3,2,1,0:T(8,128)S(1)}, u32[]{:S(2)}, u32[]{:S(2)}) collective-permute-start(f32[4,1,8,1024]{3,2,1,0:T(8,128)S(1)} %constant_dynamic-slice_fusion.2), channel_id=1, source_target_pairs={{0,4},{2,6},{4,0},{6,2},{8,12},{10,14},{12,8},{14,10},{16,20},{18,... | collective-permute-start | bytes 393224 | tf_op jit(solution)/shard_map/ppermute | solution.py:356
  144.5 4.3 %collective-permute-start.7 = (f32[2,1,8,1024]{3,2,1,0:T(8,128)S(1)}, f32[2,1,8,1024]{3,2,1,0:T(8,128)S(1)}, u32[]{:S(2)}, u32[]{:S(2)}) collective-permute-start(f32[2,1,8,1024]{3,2,1,0:T(8,128)S(1)} %constant_dynamic-slice_fusion.5), channel_id=1, source_target_pairs={{0,8},{2,10},{4,12},{6,14},{8,0},{10,2},{12,4},{14,6},{16,24},{18,... | collective-permute-start | bytes 196616 | tf_op jit(solution)/shard_map/ppermute | solution.py:356
  147.0 4.8 %collective-permute-start.13 = (f32[2,1,8,1024]{3,2,1,0:T(8,128)S(1)}, f32[2,1,8,1024]{3,2,1,0:T(8,128)S(1)}, u32[]{:S(2)}, u32[]{:S(2)}) collective-permute-start(f32[2,1,8,1024]{3,2,1,0:T(8,128)S(1)} %constant_dynamic-slice_fusion.1), channel_id=1, source_target_pairs={{0,8},{2,10},{4,12},{6,14},{8,0},{10,2},{12,4},{14,6},{16,24},{18,... | collective-permute-start | bytes 196616 | tf_op jit(solution)/shard_map/ppermute | solution.py:356
  148.8 5.3 %collective-permute-start.8 = (f32[1,1,8,1024]{3,2,1,0:T(8,128)S(1)}, f32[1,1,8,1024]{3,2,1,0:T(8,128)S(1)}, u32[]{:S(2)}, u32[]{:S(2)}) collective-permute-start(f32[1,1,8,1024]{3,2,1,0:T(8,128)S(1)} %constant_dynamic-slice_fusion.4), channel_id=1, source_target_pairs={{0,16},{2,18},{4,20},{6,22},{8,24},{10,26},{12,28},{14,30},{16,0},... | collective-permute-start | bytes 98312 | tf_op jit(solution)/shard_map/ppermute | solution.py:356
  151.8 4.9 %collective-permute-start.14 = (f32[1,1,8,1024]{3,2,1,0:T(8,128)S(1)}, f32[1,1,8,1024]{3,2,1,0:T(8,128)S(1)}, u32[]{:S(2)}, u32[]{:S(2)}) collective-permute-start(f32[1,1,8,1024]{3,2,1,0:T(8,128)S(1)} %constant_dynamic-slice_fusion), channel_id=1, source_target_pairs={{0,16},{2,18},{4,20},{6,22},{8,24},{10,26},{12,28},{14,30},{16,0},... | collective-permute-start | bytes 98312 | tf_op jit(solution)/shard_map/ppermute | solution.py:356
where the time goes:
time: 160 us; the launch traced here: 159 us
  Pallas kernels  70.1 us (44%)
  waiting for transfers between devices  36.4 us (23%)
  starting transfers between devices  23.4 us (15%)
  other arithmetic  16.4 us (10%)
  local copies, waits for them, and re-layouts  12.1 us (8%)
    pallas_call x4, Pallas kernels, chunk_sums(): pl.pallas_call(partial(chunk_kernel, plan), out_shape=jax.ShapeDtypeStruc...  57.2 us
    ppermute x3, waiting for transfers between devices, swapped(): return lax.ppermute(block, axis, route)  25.3 us
    ppermute x12, starting transfers between devices, halved_sum(): sums = kept + lax.ppermute(sent, axis, route)  18.7 us
    ppermute x12, waiting for transfers between devices, halved_sum(): sums = kept + lax.ppermute(sent, axis, route)  11.1 us
    pallas_call x2, Pallas kernels, ordered(): pl.pallas_call(partial(order_kernel, per_block // LANES), out_shape=[like...  10.8 us
    unnamed x7, other arithmetic  7.18 us
    slice x1, local copies, waits for them, and re-layouts, sums(): left_bands[:, :, low:high]  4.69 us
    ppermute x3, starting transfers between devices, swapped(): return lax.ppermute(block, axis, route)  4.63 us
  transfers between devices with their start and end apart: 15, of which 7 were waited for; matrix products, arithmetic and copies ran while one was open for 7% of the time, Pallas kernels for 22%

commit v1 on v0

v1 whole, which is shorter than its diff:
```python
from functools import partial
import math

import jax
import jax.numpy as jnp
import numpy as np
from jax import lax
from jax.experimental import pallas as pl
from jax.experimental.pallas import tpu as pltpu
from jax.sharding import PartitionSpec as P


F32 = jnp.float32
BF16 = jnp.bfloat16
LANES = 128
SUB = 8
SPAN = 3
VMEM_MIB = 16


def swapped(block, axis, apart):
    count = lax.axis_size(axis)
    route = []
    for low in range(count):
        high = low | 1 << apart
        if high != low and high < count:
            route += [(low, high), (high, low)]
    return lax.ppermute(block, axis, route)


def dft_parts(length):
    counter = np.arange(length)
    angles = (counter[:, None] * counter[None, :] % length) * (2.0 * math.pi / length)
    return np.cos(angles), np.sin(angles)


def two_terms(table):
    high = np.asarray(table, BF16)
    return high, np.asarray(table - np.asarray(high, np.float32), BF16)


def rows_table(length):
    cosine, sine = dft_parts(length)
    return np.block([[cosine, sine], [-sine, cosine]]).astype(np.float32)


def lanes_table(length):
    cosine, sine = dft_parts(length)
    return np.block([[cosine, -sine], [sine, cosine]]).astype(np.float32)


def left_table(table):
    high, low = two_terms(table)
    return jnp.asarray(np.concatenate([high, low, high], axis=1))


def right_table(table):
    high, low = two_terms(table)
    return jnp.asarray(np.concatenate([high, high, low], axis=0))


def split(value):
    high = value.astype(BF16)
    return high, (value - high.astype(F32)).astype(BF16)


def dot(a, b):
    return jnp.dot(a, b, preferred_element_type=F32)


def taken(value, lanes):
    return jnp.take_along_axis(value, lanes, axis=1, mode="promise_in_bounds")


def turned(number, count):
    back = 0
    while count > 1:
        back, number, count = 2 * back + number % 2, number // 2, count // 2
    return back


def window(chunk, chunks, rows):
    return min(max(chunk * rows // chunks - 1, 0), rows - min(SPAN, rows))


def half_planes(pairs, planes):
    return planes // 2 if pairs < SUB and planes % 2 == 0 else planes


def chunk_kernel(
    plan, near_ref, left_ref, right_ref, table_y_ref, table_x_ref, picks_ref, places_ref, turns_ref,
    *rest,
):
    if plan["add"]:
        before_ref, *rest = rest
    if plan["join"]:
        other_kept_ref, other_sent_ref, *rest = rest
    out_ref, *rest = rest
    if plan["woven"] and plan["last"]:
        send_ref, *rest = rest
    skip = plan["join"]
    for part in range(skip):
        for spot in range(out_ref.shape[0]):
            out_ref[spot, part] = other_kept_ref[spot, part]
            send_ref[spot, part] = other_sent_ref[spot, part]
    h_real, h_imag, f_even, f_odd, hold_ref, *d_refs = rest
    lefts, rights, planes = plan["lefts"], plan["rights"], plan["planes"]
    pairs = lefts * rights
    halves, tiles, stride = plan["halves"], plan["tiles"], plan["stride"]
    length, groups, rows, chunks = plan["length"], plan["groups"], plan["rows"], plan["chunks"]
    wide = tiles * SUB
    left_low, right_low = plan["low"], plan["right_low"]

    def transform_rows(z, _):
        if halves == 2:
            slot = (z % tiles) * SUB + (z // tiles) * pairs
        else:
            slot = z * SUB
        for first in range(0, pairs, 2):
            d_ref = d_refs[first // 2]
            for k in range(2):
                m, n = (first + k) // lefts, (first + k) % lefts
                lanes = slice(k * LANES, (k + 1) * LANES)
                lr, li = left_ref[0, n, left_low + z], left_ref[1, n, left_low + z]
                rr, ri = right_ref[0, m, right_low + z], right_ref[1, m, right_low + z]
                for part, field in enumerate((lr * rr + li * ri, lr * ri - li * rr)):
                    high, low = split(field)
                    for copy, term in enumerate((high, high, low)):
                        base = (2 * copy + part) * length
                        d_ref[base : base + length, lanes] = term
            moved = dot(table_y_ref[...], d_ref[...])
            for k in range(2):
                spot = pl.ds(slot + first + k, length, stride=stride)
                lanes = slice(k * LANES, (k + 1) * LANES)
                h_real[spot, :] = moved[:length, lanes]
                h_imag[spot, :] = moved[length:, lanes]
        return 0

    lax.fori_loop(0, planes, transform_rows, 0)

    def transform_lanes(group, f_ref):
        spots = [pl.ds((group * rows + y) * stride, wide) for y in range(rows)]
        real = jnp.concatenate([h_real[spot, :] for spot in spots], axis=0)
        imag = jnp.concatenate([h_imag[spot, :] for spot in spots], axis=0)
        high, low = split(jnp.concatenate([real, imag], axis=1))
        moved = dot(jnp.concatenate([high, low, high], axis=1), table_x_ref[...])
        for y in range(rows):
            f_ref[y] = moved[y * wide : (y + 1) * wide]

    upper = lax.broadcasted_iota(jnp.int32, (SUB, LANES), 0) >= SUB // 2
    late = lax.broadcasted_iota(jnp.int32, (SUB, LANES), 1) >= LANES // 2
    span = plan["span"]

    def wide_row(ref, at, *k):
        return jnp.broadcast_to(ref[k + (pl.ds(at, 1), slice(None))], (SUB, LANES))

    def box(y, tile, part):
        rows_of, lanes_of = pl.ds(tile * SUB, SUB), pl.ds(part * LANES, LANES)
        return (y, rows_of, lanes_of)

    def near(chunk, at, f_ref):
        lanes = wide_row(picks_ref, at, 0)
        start = window(chunk, chunks, rows)
        apart = wide_row(picks_ref, at, 1) - start
        same = [apart == y for y in range(span)]

        def value(tile, part):
            best = taken(f_ref[box(start, tile, part)], lanes)
            for y in range(1, span):
                best = jnp.where(same[y], taken(f_ref[box(start + y, tile, part)], lanes), best)
            return best

        return value

    def far(at, f_ref):
        lanes = wide_row(picks_ref, at, 0)
        y_of = wide_row(picks_ref, at, 1)

        def value(tile, part):
            def body(y, best):
                return jnp.where(y_of == y, taken(f_ref[box(y, tile, part)], lanes), best)

            return lax.fori_loop(0, rows, body, jnp.zeros((SUB, LANES), F32))

        return value

    def picked(at, value):
        first_turn, second_turn = plan["turns"]
        turn_r, turn_i = wide_row(turns_ref, at, 0, 0), wide_row(turns_ref, at, 0, 1)
        base_r = wide_row(turns_ref, at, first_turn, 0)
        base_i = wide_row(turns_ref, at, first_turn, 1)
        if halves == 2:
            base_r = jnp.where(upper, wide_row(turns_ref, at, second_turn, 0), base_r)
            base_i = jnp.where(upper, wide_row(turns_ref, at, second_turn, 1), base_i)
        real, imag = value(tiles - 1, 0), value(tiles - 1, 1)
        for tile in reversed(range(tiles - 1)):
            real, imag = (
                real * turn_r - imag * turn_i + value(tile, 0),
                real * turn_i + imag * turn_r + value(tile, 1),
            )
        real, imag = real * base_r - imag * base_i, real * base_i + imag * base_r
        if pairs == SUB:
            found = [real, imag]
        else:
            if halves == 2:
                real = real + pltpu.roll(real, SUB // 2, 0)
                imag = imag + pltpu.roll(imag, SUB // 2, 0)
            else:
                imag = pltpu.roll(imag, SUB // 2, 0)
            found = [jnp.where(upper, imag, real)]
        if plan["add"]:
            found = [one + before_ref[at, part] for part, one in enumerate(found)]
        return found

    def moved_back(group, found):
        result = []
        for chunk in range(chunks):
            place = wide_row(places_ref, group * chunks + chunk)
            lanes, source = place % LANES, place // LANES
            parts = []
            for part in range(len(found[0])):
                best = taken(found[0][part], lanes)
                for other in range(1, chunks):
                    best = jnp.where(source == other, taken(found[other][part], lanes), best)
                parts.append(best)
            result.append(parts)
        return result

    def group_sums(group, f_ref, look):
        found = []
        for chunk in range(chunks):
            at = group * chunks + chunk
            found.append(picked(at, look(chunk, at, f_ref)))
        if not plan["last"]:
            for chunk in range(chunks):
                for part, value in enumerate(found[chunk]):
                    out_ref[group * chunks + chunk, part] = value
            return found
        return moved_back(group, found)

    def put_couple(a, firsts, seconds):
        place = pl.ds(pl.multiple_of(a * LANES, LANES), LANES)
        for chunk in range(chunks):
            for part, (one, two) in enumerate(zip(firsts[chunk], seconds[chunk])):
                spot = turned(2 * chunk, groups)
                box_of = (spot, skip + part, slice(None), place)
                out_ref[box_of] = jnp.where(late, pltpu.roll(two, LANES // 2, 1), one)
                send_ref[box_of] = jnp.where(late, two, pltpu.roll(one, LANES // 2, 1))

    def put_single(group, found):
        for chunk in range(chunks):
            for part, value in enumerate(found[chunk]):
                out_ref[group * chunks + chunk, part] = value

    @pl.when(near_ref[0] == 1)
    def _():
        if groups % 2:

            def single(group, _):
                transform_lanes(group, f_even)
                found = group_sums(group, f_even, near)
                if plan["last"]:
                    put_single(group, found)
                return 0

            lax.fori_loop(0, groups, single, 0)
            return
        transform_lanes(0, f_even)

        def couple(a, _):
            transform_lanes(2 * a + 1, f_odd)
            firsts = group_sums(2 * a, f_even, near)
            transform_lanes(jnp.minimum(2 * a + 2, groups - 1), f_even)
            seconds = group_sums(2 * a + 1, f_odd, near)
            if plan["last"]:
                if plan["woven"]:
                    put_couple(a, firsts, seconds)
                else:
                    put_single(2 * a, firsts)
                    put_single(2 * a + 1, seconds)
            return 0

        lax.fori_loop(0, groups // 2, couple, 0)

    @pl.when(near_ref[0] == 0)
    def _():
        def compute(group):
            transform_lanes(group, f_even)

            def body(chunk, _):
                at = group * chunks + chunk
                for part, value in enumerate(picked(at, far(at, f_even))):
                    hold_ref[chunk, part] = value
                return 0

            lax.fori_loop(0, chunks, body, 0)
            count = 2 if pairs == SUB else 1
            found = [[hold_ref[chunk, part] for part in range(count)] for chunk in range(chunks)]
            return moved_back(group, found) if plan["last"] else found

        if plan["last"] and plan["woven"]:

            def couple(a, _):
                firsts = compute(2 * a)
                put_couple(a, firsts, compute(2 * a + 1))
                return 0

            lax.fori_loop(0, groups // 2, couple, 0)
        else:

            def single(group, _):
                put_single(group, compute(group))
                return 0

            lax.fori_loop(0, groups, single, 0)


def is_woven(sizes):
    groups, slots = sizes
    return 2 * slots == LANES and groups % 2 == 0


def chunk_sums(left, right, tables, lists, before, join, last, sizes, spans):
    lefts, rights, length = left.shape[1], right.shape[1], left.shape[3]
    groups, slots = sizes
    low, right_low, planes, turns = spans
    pairs = lefts * rights
    tiles = half_planes(pairs, planes)
    wide = tiles * SUB
    stride = wide if tiles % 2 else wide + SUB
    parts = 2 * pairs // SUB
    chunks = groups * slots // LANES
    rows = length // groups
    operands = [left, right, *tables, *lists[1:]]
    if before is not None:
        operands.append(before)
    if join is not None and not is_woven(sizes):
        mine = chunk_sums(left, right, tables, lists, before, None, last, sizes, spans)
        return jnp.concatenate([join, mine], axis=1)
    if join is not None:
        operands += list(join)
    skip = 0 if join is None else join[0].shape[1]
    plan = dict(
        lefts=lefts, rights=rights, planes=planes, halves=planes // tiles, tiles=tiles,
        stride=stride, length=length, groups=groups, rows=rows, chunks=chunks,
        woven=is_woven(sizes), add=before is not None, last=last, span=min(SPAN, rows),
        low=low, right_low=right_low, turns=turns, join=skip,
    )
    if is_woven(sizes) and last:
        shape = (groups // 2, skip + parts, SUB, groups * slots)
    else:
        shape = (groups * chunks, parts, SUB, LANES)
    like = jax.ShapeDtypeStruct(shape, F32)
    field = pltpu.VMEM((length * stride, LANES), F32)
    group = pltpu.VMEM((rows, wide, 2 * LANES), F32)
    flops = 2 * 3 * 2 * pairs * planes * length * (2 * length) * (2 * length)
    return pl.pallas_call(
        partial(chunk_kernel, plan),
        out_shape=[like, like] if is_woven(sizes) and last else like,
        in_specs=[pl.BlockSpec(memory_space=pltpu.SMEM)]
        + [pl.BlockSpec(memory_space=pltpu.VMEM)] * len(operands),
        scratch_shapes=[field, field, group, group, pltpu.VMEM((chunks, parts, SUB, LANES), F32)]
        + [pltpu.VMEM((6 * length, 2 * LANES), BF16)] * (pairs // 2),
        compiler_params=pltpu.CompilerParams(vmem_limit_bytes=VMEM_MIB * 1024 * 1024),
        cost_estimate=pl.CostEstimate(flops=flops, bytes_accessed=4 * left.size, transcendentals=0),
    )(lists[0], *operands)


def to_owner(sums, sizes):
    if is_woven(sizes):
        return sums
    groups, slots = sizes
    parts = sums.shape[1]
    shaped = sums.reshape(groups, -1, parts, SUB, LANES)
    shaped = jnp.moveaxis(shaped, 1, 3).reshape(groups, parts, SUB, groups, slots)
    shaped = jnp.transpose(shaped, (3, 1, 2, 0, 4)).reshape(groups, parts, SUB, groups * slots)
    shaped = shaped[np.array([turned(owner, groups) for owner in range(groups)])]
    return shaped[: groups // 2], shaped[groups // 2 :]


def add_kernel(kept_ref, got_ref, *out_refs):
    share = kept_ref.shape[0] // len(out_refs)
    for k, out_ref in enumerate(out_refs):
        for one in range(share):
            out_ref[one] = kept_ref[k * share + one] + got_ref[k * share + one]


def added(kept, got, pieces):
    like = jax.ShapeDtypeStruct((kept.shape[0] // pieces,) + kept.shape[1:], F32)
    return pl.pallas_call(
        add_kernel,
        out_shape=[like] * pieces,
        compiler_params=pltpu.CompilerParams(vmem_limit_bytes=8 * 1024 * 1024),
    )(kept, got)


def grid_parts(kept, sent, axis):
    count = 2 * kept.shape[0]
    step = 0

    def moved(value, apart):
        route = [(device, device ^ apart) for device in range(count)]
        return lax.ppermute(value, axis, route)

    while kept.shape[0] > 4:
        got = moved(sent, 1 << step)
        kept, sent = added(kept, got, 2)
        step += 1
    got = moved(sent, 1 << step)
    kept, *sent = added(kept, got, kept.shape[0])
    low, high = 2 << step, 4 << step
    step += 1
    aparts = [high, low, low | high] if len(sent) == 3 else [low] * len(sent)
    return [kept] + [moved(one, apart) for one, apart in zip(sent, aparts)]


def over(value, count):
    if count & count - 1 == 0:
        return value >> count.bit_length() - 1
    return value // count


def rest_of(value, count):
    if count & count - 1 == 0:
        return value & count - 1
    return value % count


def list_kernel(
    plan, me_ref, index_ref, table_ref, near_ref, place_ref, picks_ref, places_ref, turns_ref, hold_ref
):
    groups, slots, rows, chunks = plan["groups"], plan["slots"], plan["rows"], plan["chunks"]
    length, width = plan["length"], plan["width"]
    size, lanes = index_ref.shape[1], index_ref.shape[0]
    total = groups * slots
    subs = total // size
    row = lax.broadcasted_iota(jnp.int32, (size, lanes), 0)
    lane = lax.broadcasted_iota(jnp.int32, (size, lanes), 1)
    spot = rest_of(lane, subs) * size + row
    flat_spot = rest_of(row, subs) * size + lane
    me = me_ref[0]

    def sort(value):
        span = 2
        while span <= total:
            apart = span // 2
            rising = spot & span == 0
            while apart > 0:
                first = spot & apart == 0
                if apart < size:
                    axis, shift, full = 0, apart, size
                else:
                    axis, shift, full = 1, apart // size, lanes
                other = jnp.where(
                    first, pltpu.roll(value, full - shift, axis), pltpu.roll(value, shift, axis)
                )
                small, large = jnp.minimum(value, other), jnp.maximum(value, other)
                value = jnp.where(first == rising, small, large)
                apart //= 2
            span *= 2
        return value

    index = index_ref[...]
    wave_z = over(index, length * width)
    wave_y = rest_of(over(index, width), length)
    wave_x = rest_of(index, width)
    key = ((wave_y * length + wave_z) * width + wave_x) * total + flat_spot
    key = key.T
    hold_ref[...] = key.T
    mine = pltpu.roll(key, lanes - me * subs, 1)
    for sub in range(subs):
        own = jnp.broadcast_to(hold_ref[pl.ds(me * subs + sub, 1), :], (SUB, lanes))
        count = jnp.zeros((SUB, lanes), jnp.int32)
        for other in range(subs):
            column = jnp.broadcast_to(mine[:, other : other + 1], (size, lanes))
            for low in range(0, size, SUB):
                count = count + (column[low : low + SUB] < own).astype(jnp.int32)
        place_ref[:, sub * size : (sub + 1) * size] = jnp.sum(count, axis=0, keepdims=True)

    hold_ref[...] = over(sort(key), total).T
    if slots == 1:
        key = hold_ref[...]
    else:
        half = size // 2
        late = lax.broadcasted_iota(jnp.int32, (groups // 2, size), 1) >= half
        for pair in range(groups // 2):
            even = hold_ref[pl.ds(pair, groups // 2, stride=2 * subs), :]
            odd = hold_ref[pl.ds(subs + pair, groups // 2, stride=2 * subs), :]
            low = jnp.where(late, pltpu.roll(odd, half, 1), even)
            high = jnp.where(late, odd, pltpu.roll(even, half, 1))
            places_ref[pl.ds(2 * pair * subs, subs), :] = low
            places_ref[pl.ds((2 * pair + 1) * subs, subs), :] = high
        key = places_ref[...].T
    key = sort(rest_of(key, rows * length * width) * total + spot)
    hold_ref[...] = rest_of(sort(rest_of(key, total) * total + spot), total).T
    sharing = LANES // slots
    swap = lax.broadcasted_iota(jnp.int32, (groups, LANES), 1) ^ (rest_of(me, sharing) * slots)
    for chunk in range(chunks):
        other = chunk ^ over(me, sharing)
        value = hold_ref[pl.ds(other, groups, stride=chunks), :] if chunks > 1 else hold_ref[...]
        value = jnp.concatenate(
            [
                taken(value[low : low + SUB], swap[low : low + SUB])
                for low in range(0, groups, SUB)
            ],
            axis=0,
        )
        if chunks > 1:
            places_ref[pl.ds(chunk, groups, stride=chunks), :] = value
        else:
            places_ref[...] = value
    key = over(key, total).T
    row_of = over(key, width * length)
    chunk = rest_of(row, chunks)
    start = jnp.zeros_like(row)
    for k in range(chunks):
        start = jnp.where(chunk == k, window(k, chunks, rows), start)
    apart = row_of - start
    outside = (apart < 0) | (apart >= SPAN)
    near_ref[0] = 1 - jnp.max(outside.astype(F32)).astype(jnp.int32)
    picks_ref[0] = rest_of(key, width)
    picks_ref[1] = row_of
    wave_z = rest_of(over(key, width), length)
    cosine, sine = table_ref[0:1, :], table_ref[1:2, :]
    for k, offset in enumerate(plan["offsets"]):
        plane = 1 if k == 0 else me * plan["planes"] + offset
        angle = rest_of(wave_z * plane, length)
        for low in range(0, lanes, SUB):
            at = angle[low : low + SUB]
            turns_ref[k, 0, low : low + SUB] = taken(jnp.broadcast_to(cosine, (SUB, length)), at)
            turns_ref[k, 1, low : low + SUB] = taken(jnp.broadcast_to(sine, (SUB, length)), at)


def listed(sphere_index, me, length, width, planes, sizes, offsets):
    groups, slots = sizes
    total = groups * slots
    shape = (sphere_index.size // LANES, LANES)
    plan = dict(
        groups=groups, slots=slots, rows=length // groups, chunks=total // LANES, length=length,
        width=width, planes=planes, offsets=offsets,
    )
    counter = np.arange(length) * (2.0 * math.pi / length)
    table = jnp.asarray(np.stack([np.cos(counter), -np.sin(counter)]), F32)
    spec, small = pl.BlockSpec(memory_space=pltpu.VMEM), pl.BlockSpec(memory_space=pltpu.SMEM)
    whole = jax.ShapeDtypeStruct(shape, jnp.int32)
    return pl.pallas_call(
        partial(list_kernel, plan),
        out_shape=[
            jax.ShapeDtypeStruct((1,), jnp.int32),
            jax.ShapeDtypeStruct((1, total), jnp.int32),
            jax.ShapeDtypeStruct((2,) + shape, jnp.int32),
            whole,
            jax.ShapeDtypeStruct((len(offsets), 2) + shape, F32),
        ],
        in_specs=[small, spec, spec],
        out_specs=[small, spec, spec, spec, spec],
        scratch_shapes=[pltpu.VMEM(shape, jnp.int32)],
        cost_estimate=pl.CostEstimate(flops=10**10, bytes_accessed=10**6, transcendentals=0),
        compiler_params=pltpu.CompilerParams(vmem_limit_bytes=8 * 1024 * 1024),
    )(me.reshape(1).astype(jnp.int32), sphere_index.reshape(shape), table)


def finish_kernel(scale, count, order_ref, place_ref, *rest):
    out_ref, hold_ref = rest[2 * count], rest[2 * count + 1]
    length = out_ref.shape[-1]
    lefts = out_ref.shape[1]
    half = SUB // 2
    rights = 0
    for refs in (rest[:count], rest[count : 2 * count]):
        parts = []
        for part in range(refs[0].shape[1]):
            value = refs[0][0, part]
            for ref in refs[1:]:
                value = value + ref[0, part]
            parts.append(value * scale)
        if len(parts) > 1:
            real, imag, *parts = parts
            for m in range(SUB // lefts):
                rows = slice(m * lefts, (m + 1) * lefts)
                hold_ref[rights + m] = jnp.concatenate([real[rows], imag[rows]], axis=0)
            rights += SUB // lefts
        for part in parts:
            hold_ref[rights] = part
            rights += 1
    pieces = length // LANES
    for j in range(out_ref.shape[2]):
        block = hold_ref[order_ref[j]]
        for piece in range(pieces):
            lanes = slice(piece * LANES, (piece + 1) * LANES)
            place = jnp.broadcast_to(place_ref[:, lanes], (SUB, LANES))
            inner = place % LANES
            outer = place // LANES
            best = taken(block[:, :LANES], inner)
            for source in range(1, pieces):
                more = taken(block[:, source * LANES : (source + 1) * LANES], inner)
                best = jnp.where(outer == source, more, best)
            for n in range(lefts):
                out_ref[0, n, j : j + 1, lanes] = best[n : n + 1]
                out_ref[1, n, j : j + 1, lanes] = best[half + n : half + n + 1]


def finished(own, others, order, place, shape, scale):
    return pl.pallas_call(
        partial(finish_kernel, scale, len(own)),
        out_shape=jax.ShapeDtypeStruct(shape, F32),
        in_specs=[pl.BlockSpec(memory_space=pltpu.SMEM)]
        + [pl.BlockSpec(memory_space=pltpu.VMEM)] * (1 + 2 * len(own)),
        scratch_shapes=[pltpu.VMEM((shape[2], SUB, shape[-1]), F32)],
        compiler_params=pltpu.CompilerParams(vmem_limit_bytes=8 * 1024 * 1024),
    )(order, place, *own, *others)


def local(left_bands, right_bands, sphere_index, right_order):
    lefts, own_rights, planes = left_bands.shape[1], right_bands.shape[1], left_bands.shape[2]
    length, width = left_bands.shape[3], left_bands.shape[4]
    groups = lax.axis_size("grid")
    me = lax.axis_index("grid")
    per_block = sphere_index.shape[0] // groups
    slots = per_block // groups
    sizes = (groups, slots)
    cut = planes // 2
    ends = [(0, cut), (cut, planes)] if cut else [(0, planes)]
    routes = [(slice(0, own_rights - 1), 0, planes)]
    routes += [(slice(own_rights - 1, own_rights), low, high) for low, high in ends]
    sent = []
    for bands, low, high in routes:
        sent.append(swapped(right_bands[:, bands, low:high], "band", 0))

    marks = {None: 0}
    spans = []
    for bands, low, high in [(slice(0, own_rights), 0, planes)] + routes:
        pairs = lefts * (bands.stop - bands.start)
        half = low + half_planes(pairs, high - low)
        turns = []
        for plane in (low, half if half < high else low):
            turns.append(marks.setdefault(plane, len(marks)))
        spans.append((low, 0, high - low, tuple(turns)))
    offsets = tuple(marks)
    near, place, *lists = listed(
        sphere_index, me, length, width, planes, sizes, offsets
    )
    lists = (near, *lists)
    tables = (left_table(rows_table(length)), right_table(lanes_table(width)))

    def sums(right, span, before, join, last):
        return chunk_sums(left_bands, right, tables, lists, before, join, last, sizes, span)

    def owned(value):
        return grid_parts(*to_owner(value, sizes), "grid")

    early = sums(right_bands, spans[0], None, None, True)
    right, _ = lax.optimization_barrier((sent[0], early))
    early = ahead = sums(right, spans[1], None, early, True)
    final = None
    for k in range(1, len(sent)):
        right, _ = lax.optimization_barrier((sent[k], ahead))
        ahead = final = sums(right, spans[1 + k], final, None, k + 1 == len(sent))
    early = owned(early)
    final = owned(final)
    order = (right_order - lax.axis_index("band") * own_rights) % right_order.shape[0]
    shape = (2, lefts, right_order.shape[0], per_block)
    scale = 1.0 / (length * length * width) ** 0.5
    return finished(early, final, order, place, shape, scale)


def solution(mesh):
    placed = (P(None, "band", "grid", None, None), P(None, "band", "grid", None, None), P(), P())
    return jax.shard_map(
        local, mesh=mesh, in_specs=placed, out_specs=P(None, "band", None, "grid"), check_vma=False
    )
```

time: 160 us -> 102 us (0.64)
  other arithmetic: 16.4 us -> 0.01 us
  waiting for transfers between devices: 36.4 us -> 22.9 us
  Pallas kernels: 70.1 us -> 57.7 us
  local copies, waits for them, and re-layouts: 12.1 us -> 3.4 us
  starting transfers between devices: 23.4 us -> 17.7 us
    ppermute x3, waiting for transfers between devices: 25.3 us -> 5.51 us  [swapped(): return lax.ppermute(block, axis, route)]
    pallas_call x7 -> x10, Pallas kernels: 70.1 us -> 57.7 us  [the longest x4 49.4 us: chunk_sums(): pl.pallas_call(partial(chunk_kernel, plan), out_shape=[like, like] if is_...]
    unnamed x7 -> x0, other arithmetic: 7.18 us -> none
    ppermute x12 -> x10, waiting for transfers between devices: 11.1 us -> 17.3 us  [moved(): return lax.ppermute(value, axis, route)]
    ppermute x12 -> x10, starting transfers between devices: 18.7 us -> 12.6 us  [moved(): return lax.ppermute(value, axis, route)]
    dynamic_slice x13 -> x0, local copies, waits for them, and re-layouts: 3.75 us -> none  [the longest x12 3.16 us: halved_sum(): sent = lax.dynamic_slice_in_dim(sums, (1 - side) * half, half, 0)]
    add x13 -> x0, other arithmetic: 3.22 us -> none  [the longest x12 3.07 us: halved_sum(): sums = kept + lax.ppermute(sent, axis, route)]
    another operation x4 -> x0, other arithmetic: 2.52 us -> none  [the longest x2 1.67 us: local(): picks = jnp.stack([key % width, row_of])]
  transfers between devices with their start and end apart: 15 -> 13, of which waited for: 7 -> 4; matrix products, arithmetic and copies ran while one was open for 7% -> 1% of each run, Pallas kernels for 22% -> 55%
where the time goes in v1:
time: 102 us
  Pallas kernels  57.7 us (57%)
  waiting for transfers between devices  22.9 us (22%)
  starting transfers between devices  17.7 us (17%)
  local copies, waits for them, and re-layouts  3.4 us (3%)
    pallas_call x4, Pallas kernels, chunk_sums(): pl.pallas_call(partial(chunk_kernel, plan), out_shape=[like, like] if is_...  49.4 us
    ppermute x10, waiting for transfers between devices, moved(): return lax.ppermute(value, axis, route)  17.3 us
    ppermute x10, starting transfers between devices, moved(): return lax.ppermute(value, axis, route)  12.6 us
    pallas_call x1, Pallas kernels, listed(): pl.pallas_call(partial(list_kernel, plan), out_shape=[jax.ShapeDtypeStruc...  6.46 us
    ppermute x3, waiting for transfers between devices, swapped(): return lax.ppermute(block, axis, route)  5.51 us
    ppermute x3, starting transfers between devices, swapped(): return lax.ppermute(block, axis, route)  5.08 us
    slice x2, local copies, waits for them, and re-layouts, local(): sent.append(swapped(right_bands[:, bands, low:high], 'band', 0))  3.37 us
  transfers between devices with their start and end apart: 13, of which 4 were waited for; matrix products, arithmetic and copies ran while one was open for 1% of the time, Pallas kernels for 55%

profile of v1, /device:TPU:0, one launch (start us, length us, event | category | flops | bytes accessed | tf_op | source)
XLA Modules:
  0.0 101.8 jit_solution(8250304780575464378)
XLA Ops:
  0.0 2.5 %slice.9 = f32[2,1,8,128,128]{4,3,2,1,0:T(8,128)} slice(f32[2,2,8,128,128]{4,3,2,1,0:T(8,128)} %right_ref.1), slice={[0:2], [0:1], [0:8], [0:128], [0:128]} | slice | bytes 2097152 | tf_op jit(solution)/shard_map/slice | solution.py:627
  2.5 3.0 %collective-permute-start = (f32[2,1,8,128,128]{4,3,2,1,0:T(8,128)}, f32[2,1,8,128,128]{4,3,2,1,0:T(8,128)}, u32[]{:S(2)}, u32[]{:S(2)}) collective-permute-start(f32[2,1,8,128,128]{4,3,2,1,0:T(8,128)} %slice.9), channel_id=1, source_target_pairs={{0,1},{1,0},{2,3},{3,2},{4,5},{5,4},{6,7},{7,6},{8,9},{9,8},{10,11... | collective-permute-start | bytes 3145736 | tf_op jit(solution)/shard_map/ppermute | solution.py:28
  5.5 0.9 fusion.1
  6.4 6.5 %shard_map.73 = (s32[1]{0:T(128)}, s32[1,1024]{1,0:T(1,128)S(1)}, s32[2,128,128]{2,1,0:T(8,128)S(1)}, s32[128,128]{1,0:T(8,128)S(1)}, f32[5,2,128,128]{3,2,1,0:T(8,128)S(1)}) custom-call(s32[1]{0:T(128)} %bitcast.me_ref, s32[128,128]{1,0:T(8,128)S(1)} %bitcast.2, f32[2,128]{1,0:T(2,128)S(1)} %copy-done.5), custom_call_target="tpu_custom_call" | custom-call | flops 10000000000 | bytes 1000000 | tf_op jit(solution)/shard_map/pallas_call | solution.py:546
  12.9 19.2 %shard_map.74 = (f32[8,2,8,1024]{3,2,1,0:T(8,128)S(1)}, f32[8,2,8,1024]{3,2,1,0:T(8,128)S(1)}) custom-call(s32[1]{0:T(128)} %get-tuple-element.32.near_ref, f32[2,4,8,128,128]{4,3,2,1,0:T(8,128)S(1)} %copy-done, f32[2,2,8,128,128]{4,3,2,1,0:T(8,128)S(1)} %copy-done.1, bf16[256,768]{1,0:T(8,128)(2,1)S(1)} %copy-done.2, bf16[768,256]{1,0:T(8,128)(2,1)S(1)} %copy-done.3, ...), custom_call_target="tpu_custom_call" | custom-call | flops 6442450944 | bytes 4194304 | tf_op jit(solution)/shard_map/pallas_call | solution.py:357
  32.1 14.1 %shard_map.75 = (f32[8,3,8,1024]{3,2,1,0:T(8,128)S(1)}, f32[8,3,8,1024]{3,2,1,0:T(8,128)S(1)}) custom-call(s32[1]{0:T(128)} %get-tuple-element.32.near_ref, f32[2,4,8,128,128]{4,3,2,1,0:T(8,128)S(1)} %copy-done, f32[2,1,8,128,128]{4,3,2,1,0:T(8,128)} %collective-permute-done.right_ref, bf16[256,768]{1,0:T(8,128)(2,1)S(1)} %copy-done.2, ...), custom_call_target="tpu_custom_call" | custom-call | flops 3221225472 | bytes 4194304 | tf_op jit(solution)/shard_map/pallas_call | solution.py:357
  46.3 0.1 collective-permute-start.1
  46.3 2.1 %collective-permute-start.6 = (f32[2,1,4,128,128]{4,3,2,1,0:T(8,128)S(1)}, f32[2,1,4,128,128]{4,3,2,1,0:T(8,128)S(1)}, u32[]{:S(2)}, u32[]{:S(2)}) collective-permute-start(f32[2,1,4,128,128]{4,3,2,1,0:T(8,128)S(1)} %get-tuple-element.58), channel_id=1, source_target_pairs={{0,1},{1,0},{2,3},{3,2},{4,5},{5,4},{6,7},{7,6},{8,9},{9,8},{10,11... | collective-permute-start | bytes 1572872 | tf_op jit(solution)/shard_map/ppermute | solution.py:28
  48.4 7.0 %shard_map.78.rest_0_ = f32[128,1,8,128]{3,2,1,0:T(8,128)S(1)} custom-call(s32[1]{0:T(128)} %get-tuple-element.32.near_ref, f32[2,4,8,128,128]{4,3,2,1,0:T(8,128)S(1)} %copy-done, f32[2,1,4,128,128]{4,3,2,1,0:T(8,128)S(1)} %collective-permute-done.7.right_ref, bf16[256,768]{1,0:T(8,128)(2,1)S(1)} %copy-done.2, bf16[768,256]{1,0:T(8,128)(2,1)S(1)} %copy-done.3, ...), custom_call_target="tpu_custom_call" | custom-call | flops 1610612736 | bytes 4194304 | tf_op jit(solution)/shard_map/pallas_call | solution.py:357
  55.4 5.5 %collective-permute-done.6.right_ref = f32[2,1,4,128,128]{4,3,2,1,0:T(8,128)S(1)} collective-permute-done((f32[2,1,4,128,128]{4,3,2,1,0:T(8,128)S(1)}, f32[2,1,4,128,128]{4,3,2,1,0:T(8,128)S(1)}, u32[]{:S(2)}, u32[]{:S(2)}) %collective-permute-start.6) | collective-permute-done | bytes 524320 | tf_op jit(solution)/shard_map/ppermute | solution.py:28
  60.9 9.1 %shard_map.79 = (f32[8,1,8,1024]{3,2,1,0:T(8,128)S(1)}, f32[8,1,8,1024]{3,2,1,0:T(8,128)S(1)}) custom-call(s32[1]{0:T(128)} %get-tuple-element.32.near_ref, f32[2,4,8,128,128]{4,3,2,1,0:T(8,128)S(1)} %copy-done, f32[2,1,4,128,128]{4,3,2,1,0:T(8,128)S(1)} %collective-permute-done.6.right_ref, bf16[256,768]{1,0:T(8,128)(2,1)S(1)} %copy-done.2, ...), custom_call_target="tpu_custom_call" | custom-call | flops 1610612736 | bytes 4194304 | tf_op jit(solution)/shard_map/pallas_call | solution.py:357
  70.0 0.1 collective-permute-start.8
  70.1 0.1 shard_map.76
  70.2 1.8 %collective-permute-start.2 = (f32[4,3,8,1024]{3,2,1,0:T(8,128)S(1)}, f32[4,3,8,1024]{3,2,1,0:T(8,128)S(1)}, u32[]{:S(2)}, u32[]{:S(2)}) collective-permute-start(f32[4,3,8,1024]{3,2,1,0:T(8,128)S(1)} %get-tuple-element.42), channel_id=1, source_target_pairs={{0,4},{2,6},{4,0},{6,2},{8,12},{10,14},{12,8},{14,10},{16,20},{18,... | collective-permute-start | bytes 1179656 | tf_op jit(solution)/shard_map/ppermute | solution.py:403
  72.0 1.4 %collective-permute-start.9 = (f32[4,1,8,1024]{3,2,1,0:T(8,128)S(1)}, f32[4,1,8,1024]{3,2,1,0:T(8,128)S(1)}, u32[]{:S(2)}, u32[]{:S(2)}) collective-permute-start(f32[4,1,8,1024]{3,2,1,0:T(8,128)S(1)} %get-tuple-element.52), channel_id=1, source_target_pairs={{0,4},{2,6},{4,0},{6,2},{8,12},{10,14},{12,8},{14,10},{16,20},{18,... | collective-permute-start | bytes 393224 | tf_op jit(solution)/shard_map/ppermute | solution.py:403
  73.4 11.1 %collective-permute-done.9.got_ref = f32[4,1,8,1024]{3,2,1,0:T(8,128)S(1)} collective-permute-done((f32[4,1,8,1024]{3,2,1,0:T(8,128)S(1)}, f32[4,1,8,1024]{3,2,1,0:T(8,128)S(1)}, u32[]{:S(2)}, u32[]{:S(2)}) %collective-permute-start.9) | collective-permute-done | bytes 131104 | tf_op jit(solution)/shard_map/ppermute | solution.py:403
  84.5 2.9 %collective-permute-start.10 = (f32[1,1,8,1024]{3,2,1,0:T(8,128)S(1)}, f32[1,1,8,1024]{3,2,1,0:T(8,128)S(1)}, u32[]{:S(2)}, u32[]{:S(2)}) collective-permute-start(f32[1,1,8,1024]{3,2,1,0:T(8,128)S(1)} %get-tuple-element.54), channel_id=1, source_target_pairs={{0,16},{2,18},{4,20},{6,22},{8,24},{10,26},{12,28},{14,30},{16,0},... | collective-permute-start | bytes 98312 | tf_op jit(solution)/shard_map/ppermute | solution.py:403
  87.4 1.6 %collective-permute-start.11 = (f32[1,1,8,1024]{3,2,1,0:T(8,128)S(1)}, f32[1,1,8,1024]{3,2,1,0:T(8,128)S(1)}, u32[]{:S(2)}, u32[]{:S(2)}) collective-permute-start(f32[1,1,8,1024]{3,2,1,0:T(8,128)S(1)} %get-tuple-element.55), channel_id=1, source_target_pairs={{0,8},{2,10},{4,12},{6,14},{8,0},{10,2},{12,4},{14,6},{16,24},{18,... | collective-permute-start | bytes 98312 | tf_op jit(solution)/shard_map/ppermute | solution.py:403
  89.1 2.0 %collective-permute-start.3 = (f32[1,3,8,1024]{3,2,1,0:T(8,128)S(1)}, f32[1,3,8,1024]{3,2,1,0:T(8,128)S(1)}, u32[]{:S(2)}, u32[]{:S(2)}) collective-permute-start(f32[1,3,8,1024]{3,2,1,0:T(8,128)S(1)} %get-tuple-element.44), channel_id=1, source_target_pairs={{0,16},{2,18},{4,20},{6,22},{8,24},{10,26},{12,28},{14,30},{16,0},... | collective-permute-start | bytes 294920 | tf_op jit(solution)/shard_map/ppermute | solution.py:403
  91.0 2.5 %collective-permute-start.4 = (f32[1,3,8,1024]{3,2,1,0:T(8,128)S(1)}, f32[1,3,8,1024]{3,2,1,0:T(8,128)S(1)}, u32[]{:S(2)}, u32[]{:S(2)}) collective-permute-start(f32[1,3,8,1024]{3,2,1,0:T(8,128)S(1)} %get-tuple-element.45), channel_id=1, source_target_pairs={{0,8},{2,10},{4,12},{6,14},{8,0},{10,2},{12,4},{14,6},{16,24},{18,... | collective-permute-start | bytes 294920 | tf_op jit(solution)/shard_map/ppermute | solution.py:403
  93.5 0.4 collective-permute-start.5
  93.9 1.1 %collective-permute-done.12.rest_7_ = f32[1,1,8,1024]{3,2,1,0:T(8,128)S(1)} collective-permute-done((f32[1,1,8,1024]{3,2,1,0:T(8,128)S(1)}, f32[1,1,8,1024]{3,2,1,0:T(8,128)S(1)}, u32[]{:S(2)}, u32[]{:S(2)}) %collective-permute-start.12) | collective-permute-done | bytes 32800 | tf_op jit(solution)/shard_map/ppermute | solution.py:403
  95.1 5.0 %collective-permute-done.3.rest_1_ = f32[1,3,8,1024]{3,2,1,0:T(8,128)S(1)} collective-permute-done((f32[1,3,8,1024]{3,2,1,0:T(8,128)S(1)}, f32[1,3,8,1024]{3,2,1,0:T(8,128)S(1)}, u32[]{:S(2)}, u32[]{:S(2)}) %collective-permute-start.3) | collective-permute-done | bytes 98336 | tf_op jit(solution)/shard_map/ppermute | solution.py:403
  100.1 1.7 %shard_map.82 = f32[2,4,4,1024]{3,2,1,0:T(4,128)} custom-call(s32[4]{0:T(128)S(1)} %and_select_fusion.order_ref, s32[1,1024]{1,0:T(1,128)S(1)} %get-tuple-element.31.place_ref, f32[1,3,8,1024]{3,2,1,0:T(8,128)S(1)} %get-tuple-element.43.rest_0_, f32[1,3,8,1024]{3,2,1,0:T(8,128)S(1)} %collective-permute-done.3.rest_1_, ...), custom_call_target="tpu_custom_call" | custom-call | tf_op jit(solution)/shard_map/pallas_call | solution.py:603
  (29 shorter events, 0.2 us)
Async XLA Ops:
  0.0 5.5 %copy-start.1 = (f32[2,2,8,128,128]{4,3,2,1,0:T(8,128)S(1)}, f32[2,2,8,128,128]{4,3,2,1,0:T(8,128)}, u32[]{:S(2)}) copy-start(f32[2,2,8,128,128]{4,3,2,1,0:T(8,128)} %right_ref.1) | copy-start | bytes 6291460
  0.0 6.4 %copy-start.5 = (f32[2,128]{1,0:T(2,128)S(1)}, f32[2,128]{1,0:T(2,128)}, u32[]{:S(2)}) copy-start(f32[2,128]{1,0:T(2,128)} %constant.31.clone.table_ref) | copy-start | bytes 3076
  0.0 6.4 %copy-start.4 = (s32[16384]{0:T(1024)S(1)}, s32[16384]{0:T(1024)}, u32[]{:S(2)}) copy-start(s32[16384]{0:T(1024)} %param.9) | copy-start | bytes 196612
  2.5 29.6 %collective-permute-start = (f32[2,1,8,128,128]{4,3,2,1,0:T(8,128)}, f32[2,1,8,128,128]{4,3,2,1,0:T(8,128)}, u32[]{:S(2)}, u32[]{:S(2)}) collective-permute-start(f32[2,1,8,128,128]{4,3,2,1,0:T(8,128)} %slice.9), channel_id=1, source_target_pairs={{0,1},{1,0},{2,3},{3,2},{4,5},{5,4},{6,7},{7,6},{8,9},{9,8},{10,11... | collective-permute-start | bytes 3145736 | tf_op jit(solution)/shard_map/ppermute | solution.py:28
  6.4 42.0 %collective-permute-start.7 = (f32[2,1,4,128,128]{4,3,2,1,0:T(8,128)}, f32[2,1,4,128,128]{4,3,2,1,0:T(8,128)S(1)}, u32[]{:S(2)}, u32[]{:S(2)}) collective-permute-start(f32[2,1,4,128,128]{4,3,2,1,0:T(8,128)} %get-tuple-element.57), channel_id=1, source_target_pairs={{0,1},{1,0},{2,3},{3,2},{4,5},{5,4},{6,7},{7,6},{8,9},{9,8},{10,11... | collective-permute-start | bytes 1572872 | tf_op jit(solution)/shard_map/ppermute | solution.py:28
  6.4 6.5 %copy-start = (f32[2,4,8,128,128]{4,3,2,1,0:T(8,128)S(1)}, f32[2,4,8,128,128]{4,3,2,1,0:T(8,128)}, u32[]{:S(2)}) copy-start(f32[2,4,8,128,128]{4,3,2,1,0:T(8,128)} %left_ref.7) | copy-start | bytes 12582916
  6.4 6.5 %copy-start.2 = (bf16[256,768]{1,0:T(8,128)(2,1)S(1)}, bf16[256,768]{1,0:T(8,128)(2,1)}, u32[]{:S(2)}) copy-start(bf16[256,768]{1,0:T(8,128)(2,1)} %constant.32.clone.table_y_ref) | copy-start | bytes 1179652
  6.4 6.5 %copy-start.3 = (bf16[768,256]{1,0:T(8,128)(2,1)S(1)}, bf16[768,256]{1,0:T(8,128)(2,1)}, u32[]{:S(2)}) copy-start(bf16[768,256]{1,0:T(8,128)(2,1)} %constant.33.clone.table_x_ref) | copy-start | bytes 1179652
  46.3 23.8 %collective-permute-start.1 = (f32[8,3,8,1024]{3,2,1,0:T(8,128)S(1)}, f32[8,3,8,1024]{3,2,1,0:T(8,128)S(1)}, u32[]{:S(2)}, u32[]{:S(2)}) collective-permute-start(f32[8,3,8,1024]{3,2,1,0:T(8,128)S(1)} %get-tuple-element.40), channel_id=1, source_target_pairs={{0,2},{2,0},{4,6},{6,4},{8,10},{10,8},{12,14},{14,12},{16,18},{18,... | collective-permute-start | bytes 2359304 | tf_op jit(solution)/shard_map/ppermute | solution.py:403
  46.3 14.6 %collective-permute-start.6 = (f32[2,1,4,128,128]{4,3,2,1,0:T(8,128)S(1)}, f32[2,1,4,128,128]{4,3,2,1,0:T(8,128)S(1)}, u32[]{:S(2)}, u32[]{:S(2)}) collective-permute-start(f32[2,1,4,128,128]{4,3,2,1,0:T(8,128)S(1)} %get-tuple-element.58), channel_id=1, source_target_pairs={{0,1},{1,0},{2,3},{3,2},{4,5},{5,4},{6,7},{7,6},{8,9},{9,8},{10,11... | collective-permute-start | bytes 1572872 | tf_op jit(solution)/shard_map/ppermute | solution.py:28
  70.0 23.9 %copy-start.6 = (s32[4]{0:T(128)S(1)}, s32[4]{0:T(128)}, u32[]{:S(2)}) copy-start(s32[4]{0:T(128)} %param.10) | copy-start | bytes 52
  70.0 2.0 %collective-permute-start.8 = (f32[8,1,8,1024]{3,2,1,0:T(8,128)S(1)}, f32[8,1,8,1024]{3,2,1,0:T(8,128)S(1)}, u32[]{:S(2)}, u32[]{:S(2)}) collective-permute-start(f32[8,1,8,1024]{3,2,1,0:T(8,128)S(1)} %get-tuple-element.50), channel_id=1, source_target_pairs={{0,2},{2,0},{4,6},{6,4},{8,10},{10,8},{12,14},{14,12},{16,18},{18,... | collective-permute-start | bytes 786440 | tf_op jit(solution)/shard_map/ppermute | solution.py:403
  70.2 18.9 %collective-permute-start.2 = (f32[4,3,8,1024]{3,2,1,0:T(8,128)S(1)}, f32[4,3,8,1024]{3,2,1,0:T(8,128)S(1)}, u32[]{:S(2)}, u32[]{:S(2)}) collective-permute-start(f32[4,3,8,1024]{3,2,1,0:T(8,128)S(1)} %get-tuple-element.42), channel_id=1, source_target_pairs={{0,4},{2,6},{4,0},{6,2},{8,12},{10,14},{12,8},{14,10},{16,20},{18,... | collective-permute-start | bytes 1179656 | tf_op jit(solution)/shard_map/ppermute | solution.py:403
  72.0 12.6 %collective-permute-start.9 = (f32[4,1,8,1024]{3,2,1,0:T(8,128)S(1)}, f32[4,1,8,1024]{3,2,1,0:T(8,128)S(1)}, u32[]{:S(2)}, u32[]{:S(2)}) collective-permute-start(f32[4,1,8,1024]{3,2,1,0:T(8,128)S(1)} %get-tuple-element.52), channel_id=1, source_target_pairs={{0,4},{2,6},{4,0},{6,2},{8,12},{10,14},{12,8},{14,10},{16,20},{18,... | collective-permute-start | bytes 393224 | tf_op jit(solution)/shard_map/ppermute | solution.py:403
  84.5 9.0 %collective-permute-start.10 = (f32[1,1,8,1024]{3,2,1,0:T(8,128)S(1)}, f32[1,1,8,1024]{3,2,1,0:T(8,128)S(1)}, u32[]{:S(2)}, u32[]{:S(2)}) collective-permute-start(f32[1,1,8,1024]{3,2,1,0:T(8,128)S(1)} %get-tuple-element.54), channel_id=1, source_target_pairs={{0,16},{2,18},{4,20},{6,22},{8,24},{10,26},{12,28},{14,30},{16,0},... | collective-permute-start | bytes 98312 | tf_op jit(solution)/shard_map/ppermute | solution.py:403
  87.4 6.5 %collective-permute-start.11 = (f32[1,1,8,1024]{3,2,1,0:T(8,128)S(1)}, f32[1,1,8,1024]{3,2,1,0:T(8,128)S(1)}, u32[]{:S(2)}, u32[]{:S(2)}) collective-permute-start(f32[1,1,8,1024]{3,2,1,0:T(8,128)S(1)} %get-tuple-element.55), channel_id=1, source_target_pairs={{0,8},{2,10},{4,12},{6,14},{8,0},{10,2},{12,4},{14,6},{16,24},{18,... | collective-permute-start | bytes 98312 | tf_op jit(solution)/shard_map/ppermute | solution.py:403
  89.0 6.1 %collective-permute-start.12 = (f32[1,1,8,1024]{3,2,1,0:T(8,128)S(1)}, f32[1,1,8,1024]{3,2,1,0:T(8,128)S(1)}, u32[]{:S(2)}, u32[]{:S(2)}) collective-permute-start(f32[1,1,8,1024]{3,2,1,0:T(8,128)S(1)} %get-tuple-element.56), channel_id=1, source_target_pairs={{0,24},{2,26},{4,28},{6,30},{8,16},{10,18},{12,20},{14,22},{16,8},... | collective-permute-start | bytes 98312 | tf_op jit(solution)/shard_map/ppermute | solution.py:403
  89.1 11.1 %collective-permute-start.3 = (f32[1,3,8,1024]{3,2,1,0:T(8,128)S(1)}, f32[1,3,8,1024]{3,2,1,0:T(8,128)S(1)}, u32[]{:S(2)}, u32[]{:S(2)}) collective-permute-start(f32[1,3,8,1024]{3,2,1,0:T(8,128)S(1)} %get-tuple-element.44), channel_id=1, source_target_pairs={{0,16},{2,18},{4,20},{6,22},{8,24},{10,26},{12,28},{14,30},{16,0},... | collective-permute-start | bytes 294920 | tf_op jit(solution)/shard_map/ppermute | solution.py:403
  91.0 9.1 %collective-permute-start.4 = (f32[1,3,8,1024]{3,2,1,0:T(8,128)S(1)}, f32[1,3,8,1024]{3,2,1,0:T(8,128)S(1)}, u32[]{:S(2)}, u32[]{:S(2)}) collective-permute-start(f32[1,3,8,1024]{3,2,1,0:T(8,128)S(1)} %get-tuple-element.45), channel_id=1, source_target_pairs={{0,8},{2,10},{4,12},{6,14},{8,0},{10,2},{12,4},{14,6},{16,24},{18,... | collective-permute-start | bytes 294920 | tf_op jit(solution)/shard_map/ppermute | solution.py:403
  93.5 6.6 %collective-permute-start.5 = (f32[1,3,8,1024]{3,2,1,0:T(8,128)S(1)}, f32[1,3,8,1024]{3,2,1,0:T(8,128)S(1)}, u32[]{:S(2)}, u32[]{:S(2)}) collective-permute-start(f32[1,3,8,1024]{3,2,1,0:T(8,128)S(1)} %get-tuple-element.46), channel_id=1, source_target_pairs={{0,24},{2,26},{4,28},{6,30},{8,16},{10,18},{12,20},{14,22},{16,8},... | collective-permute-start | bytes 294920 | tf_op jit(solution)/shard_map/ppermute | solution.py:403

commit v2 on v1

--- a/solution.py
+++ b/solution.py
@@ -14,7 +14,6 @@
 BF16 = jnp.bfloat16
 LANES = 128
 SUB = 8
-SPAN = 3
 VMEM_MIB = 16
 
 
@@ -80,7 +79,8 @@
 
 
 def window(chunk, chunks, rows):
-    return min(max(chunk * rows // chunks - 1, 0), rows - min(SPAN, rows))
+    middle = chunk * rows // chunks
+    return max(middle - 1, 0), min(middle + 2, rows)
 
 
 def half_planes(pairs, planes):
@@ -136,7 +136,14 @@
                 h_imag[spot, :] = moved[length:, lanes]
         return 0
 
-    lax.fori_loop(0, planes, transform_rows, 0)
+    def transform_two(a, _):
+        transform_rows(2 * a, 0)
+        return transform_rows(2 * a + 1, 0)
+
+    if planes % 2 == 0 and pairs < SUB:
+        lax.fori_loop(0, planes // 2, transform_two, 0)
+    else:
+        lax.fori_loop(0, planes, transform_rows, 0)
 
     def transform_lanes(group, f_ref):
         spots = [pl.ds((group * rows + y) * stride, wide) for y in range(rows)]
@@ -149,7 +156,6 @@
 
     upper = lax.broadcasted_iota(jnp.int32, (SUB, LANES), 0) >= SUB // 2
     late = lax.broadcasted_iota(jnp.int32, (SUB, LANES), 1) >= LANES // 2
-    span = plan["span"]
 
     def wide_row(ref, at, *k):
         return jnp.broadcast_to(ref[k + (pl.ds(at, 1), slice(None))], (SUB, LANES))
@@ -160,14 +166,14 @@
 
     def near(chunk, at, f_ref):
         lanes = wide_row(picks_ref, at, 0)
-        start = window(chunk, chunks, rows)
-        apart = wide_row(picks_ref, at, 1) - start
-        same = [apart == y for y in range(span)]
+        start, end = window(chunk, chunks, rows)
+        row_of = wide_row(picks_ref, at, 1)
+        same = {y: row_of == y for y in range(start + 1, end)}
 
         def value(tile, part):
             best = taken(f_ref[box(start, tile, part)], lanes)
-            for y in range(1, span):
-                best = jnp.where(same[y], taken(f_ref[box(start + y, tile, part)], lanes), best)
+            for y in range(start + 1, end):
+                best = jnp.where(same[y], taken(f_ref[box(y, tile, part)], lanes), best)
             return best
 
         return value
@@ -280,7 +286,14 @@
                     put_single(2 * a + 1, seconds)
             return 0
 
-        lax.fori_loop(0, groups // 2, couple, 0)
+        def two_couples(a, _):
+            couple(2 * a, 0)
+            return couple(2 * a + 1, 0)
+
+        if groups % 4 == 0 and pairs < SUB:
+            lax.fori_loop(0, groups // 4, two_couples, 0)
+        else:
+            lax.fori_loop(0, groups // 2, couple, 0)
 
     @pl.when(near_ref[0] == 0)
     def _():
@@ -327,7 +340,7 @@
     pairs = lefts * rights
     tiles = half_planes(pairs, planes)
     wide = tiles * SUB
-    stride = wide if tiles % 2 else wide + SUB
+    stride = wide + SUB // 2
     parts = 2 * pairs // SUB
     chunks = groups * slots // LANES
     rows = length // groups
@@ -343,7 +356,7 @@
     plan = dict(
         lefts=lefts, rights=rights, planes=planes, halves=planes // tiles, tiles=tiles,
         stride=stride, length=length, groups=groups, rows=rows, chunks=chunks,
-        woven=is_woven(sizes), add=before is not None, last=last, span=min(SPAN, rows),
+        woven=is_woven(sizes), add=before is not None, last=last,
         low=low, right_low=right_low, turns=turns, join=skip,
     )
     if is_woven(sizes) and last:
@@ -440,25 +453,56 @@
     flat_spot = rest_of(row, subs) * size + lane
     me = me_ref[0]
 
+    inner_row = lax.broadcasted_iota(jnp.int32, (SUB, lanes), 0)
+    sub_of = rest_of(lax.broadcasted_iota(jnp.int32, (SUB, lanes), 1), subs)
+
+    def order_of(one, two, rising):
+        small, large = jnp.minimum(one, two), jnp.maximum(one, two)
+        if isinstance(rising, bool):
+            return (small, large) if rising else (large, small)
+        return jnp.where(rising, small, large), jnp.where(rising, large, small)
+
     def sort(value):
+        tiles = [value[low : low + SUB] for low in range(0, size, SUB)]
         span = 2
         while span <= total:
             apart = span // 2
-            rising = spot & span == 0
             while apart > 0:
-                first = spot & apart == 0
-                if apart < size:
-                    axis, shift, full = 0, apart, size
+                if SUB <= apart < size:
+                    step = apart // SUB
+                    for k in range(len(tiles)):
+                        if k & step == 0:
+                            if span < size:
+                                rising = k * SUB & span == 0
+                            elif span == total:
+                                rising = True
+                            else:
+                                rising = sub_of & span // size == 0
+                            tiles[k], tiles[k + step] = order_of(tiles[k], tiles[k + step], rising)
                 else:
-                    axis, shift, full = 1, apart // size, lanes
-                other = jnp.where(
-                    first, pltpu.roll(value, full - shift, axis), pltpu.roll(value, shift, axis)
-                )
-                small, large = jnp.minimum(value, other), jnp.maximum(value, other)
-                value = jnp.where(first == rising, small, large)
+                    for k, tile in enumerate(tiles):
+                        if apart < SUB:
+                            first = inner_row & apart == 0
+                            axis, shift, full = 0, apart, SUB
+                        else:
+                            first = sub_of & apart // size == 0
+                            axis, shift, full = 1, apart // size, lanes
+                        if span < SUB:
+                            least = first == (inner_row & span == 0)
+                        elif span < size:
+                            least = first if k * SUB & span == 0 else jnp.logical_not(first)
+                        elif span == total:
+                            least = first
+                        else:
+                            least = first == (sub_of & span // size == 0)
+                        other = pltpu.roll(tile, shift, axis)
+                        if 2 * shift != full:
+                            other = jnp.where(first, pltpu.roll(tile, full - shift, axis), other)
+                        small, large = jnp.minimum(tile, other), jnp.maximum(tile, other)
+                        tiles[k] = jnp.where(least, small, large)
                 apart //= 2
             span *= 2
-        return value
+        return jnp.concatenate(tiles, axis=0)
 
     index = index_ref[...]
     wave_z = over(index, length * width)
@@ -512,11 +556,11 @@
     key = over(key, total).T
     row_of = over(key, width * length)
     chunk = rest_of(row, chunks)
-    start = jnp.zeros_like(row)
+    start, end = jnp.zeros_like(row), jnp.zeros_like(row)
     for k in range(chunks):
-        start = jnp.where(chunk == k, window(k, chunks, rows), start)
-    apart = row_of - start
-    outside = (apart < 0) | (apart >= SPAN)
+        lowest, above = window(k, chunks, rows)
+        start, end = jnp.where(chunk == k, lowest, start), jnp.where(chunk == k, above, end)
+    outside = (row_of < start) | (row_of >= end)
     near_ref[0] = 1 - jnp.max(outside.astype(F32)).astype(jnp.int32)
     picks_ref[0] = rest_of(key, width)
     picks_ref[1] = row_of

time: 102 us -> 97.5 us (0.956)
  Pallas kernels: 57.7 us -> 51.7 us
  waiting for transfers between devices: 22.9 us -> 24.4 us
    pallas_call x4, Pallas kernels: 49.4 us -> 45.5 us  [chunk_sums(): pl.pallas_call(partial(chunk_kernel, plan), out_shape=[like, like] if is_...]
    pallas_call x1, Pallas kernels: 6.46 us -> 4.33 us  [listed(): pl.pallas_call(partial(list_kernel, plan), out_shape=[jax.ShapeDtypeStruc...]
    ppermute x3, waiting for transfers between devices: 5.51 us -> 7.05 us  [swapped(): return lax.ppermute(block, axis, route)]
  transfers between devices with their start and end apart: 13 -> 13, of which waited for: 4 -> 5; matrix products, arithmetic and copies ran while one was open for 1% -> 1% of each run, Pallas kernels for 55% -> 51%
where the time goes in v2:
time: 97.5 us; the launch traced here: 97.3 us
  Pallas kernels  51.7 us (53%)
  waiting for transfers between devices  24.4 us (25%)
  starting transfers between devices  17.7 us (18%)
  local copies, waits for them, and re-layouts  3.4 us (3%)
    pallas_call x4, Pallas kernels, chunk_sums(): pl.pallas_call(partial(chunk_kernel, plan), out_shape=[like, like] if is_...  45.5 us
    ppermute x10, waiting for transfers between devices, moved(): return lax.ppermute(value, axis, route)  17.3 us
    ppermute x10, starting transfers between devices, moved(): return lax.ppermute(value, axis, route)  12.6 us
    ppermute x3, waiting for transfers between devices, swapped(): return lax.ppermute(block, axis, route)  7.05 us
    ppermute x3, starting transfers between devices, swapped(): return lax.ppermute(block, axis, route)  5.09 us
    pallas_call x1, Pallas kernels, listed(): pl.pallas_call(partial(list_kernel, plan), out_shape=[jax.ShapeDtypeStruc...  4.33 us
    slice x2, local copies, waits for them, and re-layouts, local(): sent.append(swapped(right_bands[:, bands, low:high], 'band', 0))  3.37 us
  transfers between devices with their start and end apart: 13, of which 5 were waited for; matrix products, arithmetic and copies ran while one was open for 1% of the time, Pallas kernels for 51%

profile of v2, /device:TPU:0, one launch (start us, length us, event | category | flops | bytes accessed | tf_op | source)
XLA Modules:
  0.0 97.3 jit_solution(3870237072240295789)
XLA Ops:
  0.0 2.5 %slice.9 = f32[2,1,8,128,128]{4,3,2,1,0:T(8,128)} slice(f32[2,2,8,128,128]{4,3,2,1,0:T(8,128)} %right_ref.1), slice={[0:2], [0:1], [0:8], [0:128], [0:128]} | slice | bytes 2097152 | tf_op jit(solution)/shard_map/slice | solution.py:671
  2.5 3.0 %collective-permute-start = (f32[2,1,8,128,128]{4,3,2,1,0:T(8,128)}, f32[2,1,8,128,128]{4,3,2,1,0:T(8,128)}, u32[]{:S(2)}, u32[]{:S(2)}) collective-permute-start(f32[2,1,8,128,128]{4,3,2,1,0:T(8,128)} %slice.9), channel_id=1, source_target_pairs={{0,1},{1,0},{2,3},{3,2},{4,5},{5,4},{6,7},{7,6},{8,9},{9,8},{10,11... | collective-permute-start | bytes 3145736 | tf_op jit(solution)/shard_map/ppermute | solution.py:27
  5.5 0.9 fusion.1
  6.4 4.3 %shard_map.73 = (s32[1]{0:T(128)}, s32[1,1024]{1,0:T(1,128)S(1)}, s32[2,128,128]{2,1,0:T(8,128)S(1)}, s32[128,128]{1,0:T(8,128)S(1)}, f32[5,2,128,128]{3,2,1,0:T(8,128)S(1)}) custom-call(s32[1]{0:T(128)} %bitcast.me_ref, s32[128,128]{1,0:T(8,128)S(1)} %bitcast.2, f32[2,128]{1,0:T(2,128)S(1)} %copy-done.5), custom_call_target="tpu_custom_call" | custom-call | flops 10000000000 | bytes 1000000 | tf_op jit(solution)/shard_map/pallas_call | solution.py:590
  10.8 18.3 %shard_map.74 = (f32[8,2,8,1024]{3,2,1,0:T(8,128)S(1)}, f32[8,2,8,1024]{3,2,1,0:T(8,128)S(1)}) custom-call(s32[1]{0:T(128)} %get-tuple-element.32.near_ref, f32[2,4,8,128,128]{4,3,2,1,0:T(8,128)S(1)} %copy-done, f32[2,2,8,128,128]{4,3,2,1,0:T(8,128)S(1)} %copy-done.1, bf16[256,768]{1,0:T(8,128)(2,1)S(1)} %copy-done.2, bf16[768,256]{1,0:T(8,128)(2,1)S(1)} %copy-done.3, ...), custom_call_target="tpu_custom_call" | custom-call | flops 6442450944 | bytes 4194304 | tf_op jit(solution)/shard_map/pallas_call | solution.py:370
  29.1 0.7 collective-permute-done.right_ref
  29.8 12.9 %shard_map.75 = (f32[8,3,8,1024]{3,2,1,0:T(8,128)S(1)}, f32[8,3,8,1024]{3,2,1,0:T(8,128)S(1)}) custom-call(s32[1]{0:T(128)} %get-tuple-element.32.near_ref, f32[2,4,8,128,128]{4,3,2,1,0:T(8,128)S(1)} %copy-done, f32[2,1,8,128,128]{4,3,2,1,0:T(8,128)} %collective-permute-done.right_ref, bf16[256,768]{1,0:T(8,128)(2,1)S(1)} %copy-done.2, ...), custom_call_target="tpu_custom_call" | custom-call | flops 3221225472 | bytes 4194304 | tf_op jit(solution)/shard_map/pallas_call | solution.py:370
  42.8 2.1 %collective-permute-start.6 = (f32[2,1,4,128,128]{4,3,2,1,0:T(8,128)S(1)}, f32[2,1,4,128,128]{4,3,2,1,0:T(8,128)S(1)}, u32[]{:S(2)}, u32[]{:S(2)}) collective-permute-start(f32[2,1,4,128,128]{4,3,2,1,0:T(8,128)S(1)} %get-tuple-element.58), channel_id=1, source_target_pairs={{0,1},{1,0},{2,3},{3,2},{4,5},{5,4},{6,7},{7,6},{8,9},{9,8},{10,11... | collective-permute-start | bytes 1572872 | tf_op jit(solution)/shard_map/ppermute | solution.py:27
  44.9 6.2 %shard_map.78.rest_0_ = f32[128,1,8,128]{3,2,1,0:T(8,128)S(1)} custom-call(s32[1]{0:T(128)} %get-tuple-element.32.near_ref, f32[2,4,8,128,128]{4,3,2,1,0:T(8,128)S(1)} %copy-done, f32[2,1,4,128,128]{4,3,2,1,0:T(8,128)S(1)} %collective-permute-done.7.right_ref, bf16[256,768]{1,0:T(8,128)(2,1)S(1)} %copy-done.2, bf16[768,256]{1,0:T(8,128)(2,1)S(1)} %copy-done.3, ...), custom_call_target="tpu_custom_call" | custom-call | flops 1610612736 | bytes 4194304 | tf_op jit(solution)/shard_map/pallas_call | solution.py:370
  51.0 6.3 %collective-permute-done.6.right_ref = f32[2,1,4,128,128]{4,3,2,1,0:T(8,128)S(1)} collective-permute-done((f32[2,1,4,128,128]{4,3,2,1,0:T(8,128)S(1)}, f32[2,1,4,128,128]{4,3,2,1,0:T(8,128)S(1)}, u32[]{:S(2)}, u32[]{:S(2)}) %collective-permute-start.6) | collective-permute-done | bytes 524320 | tf_op jit(solution)/shard_map/ppermute | solution.py:27
  57.4 8.1 %shard_map.79 = (f32[8,1,8,1024]{3,2,1,0:T(8,128)S(1)}, f32[8,1,8,1024]{3,2,1,0:T(8,128)S(1)}) custom-call(s32[1]{0:T(128)} %get-tuple-element.32.near_ref, f32[2,4,8,128,128]{4,3,2,1,0:T(8,128)S(1)} %copy-done, f32[2,1,4,128,128]{4,3,2,1,0:T(8,128)S(1)} %collective-permute-done.6.right_ref, bf16[256,768]{1,0:T(8,128)(2,1)S(1)} %copy-done.2, ...), custom_call_target="tpu_custom_call" | custom-call | flops 1610612736 | bytes 4194304 | tf_op jit(solution)/shard_map/pallas_call | solution.py:370
  65.5 0.1 collective-permute-start.8
  65.6 0.1 shard_map.76
  65.7 1.8 %collective-permute-start.2 = (f32[4,3,8,1024]{3,2,1,0:T(8,128)S(1)}, f32[4,3,8,1024]{3,2,1,0:T(8,128)S(1)}, u32[]{:S(2)}, u32[]{:S(2)}) collective-permute-start(f32[4,3,8,1024]{3,2,1,0:T(8,128)S(1)} %get-tuple-element.42), channel_id=1, source_target_pairs={{0,4},{2,6},{4,0},{6,2},{8,12},{10,14},{12,8},{14,10},{16,20},{18,... | collective-permute-start | bytes 1179656 | tf_op jit(solution)/shard_map/ppermute | solution.py:416
  67.5 1.4 %collective-permute-start.9 = (f32[4,1,8,1024]{3,2,1,0:T(8,128)S(1)}, f32[4,1,8,1024]{3,2,1,0:T(8,128)S(1)}, u32[]{:S(2)}, u32[]{:S(2)}) collective-permute-start(f32[4,1,8,1024]{3,2,1,0:T(8,128)S(1)} %get-tuple-element.52), channel_id=1, source_target_pairs={{0,4},{2,6},{4,0},{6,2},{8,12},{10,14},{12,8},{14,10},{16,20},{18,... | collective-permute-start | bytes 393224 | tf_op jit(solution)/shard_map/ppermute | solution.py:416
  68.9 11.1 %collective-permute-done.9.got_ref = f32[4,1,8,1024]{3,2,1,0:T(8,128)S(1)} collective-permute-done((f32[4,1,8,1024]{3,2,1,0:T(8,128)S(1)}, f32[4,1,8,1024]{3,2,1,0:T(8,128)S(1)}, u32[]{:S(2)}, u32[]{:S(2)}) %collective-permute-start.9) | collective-permute-done | bytes 131104 | tf_op jit(solution)/shard_map/ppermute | solution.py:416
  80.0 2.9 %collective-permute-start.10 = (f32[1,1,8,1024]{3,2,1,0:T(8,128)S(1)}, f32[1,1,8,1024]{3,2,1,0:T(8,128)S(1)}, u32[]{:S(2)}, u32[]{:S(2)}) collective-permute-start(f32[1,1,8,1024]{3,2,1,0:T(8,128)S(1)} %get-tuple-element.54), channel_id=1, source_target_pairs={{0,16},{2,18},{4,20},{6,22},{8,24},{10,26},{12,28},{14,30},{16,0},... | collective-permute-start | bytes 98312 | tf_op jit(solution)/shard_map/ppermute | solution.py:416
  82.9 1.6 %collective-permute-start.11 = (f32[1,1,8,1024]{3,2,1,0:T(8,128)S(1)}, f32[1,1,8,1024]{3,2,1,0:T(8,128)S(1)}, u32[]{:S(2)}, u32[]{:S(2)}) collective-permute-start(f32[1,1,8,1024]{3,2,1,0:T(8,128)S(1)} %get-tuple-element.55), channel_id=1, source_target_pairs={{0,8},{2,10},{4,12},{6,14},{8,0},{10,2},{12,4},{14,6},{16,24},{18,... | collective-permute-start | bytes 98312 | tf_op jit(solution)/shard_map/ppermute | solution.py:416
  84.6 2.0 %collective-permute-start.3 = (f32[1,3,8,1024]{3,2,1,0:T(8,128)S(1)}, f32[1,3,8,1024]{3,2,1,0:T(8,128)S(1)}, u32[]{:S(2)}, u32[]{:S(2)}) collective-permute-start(f32[1,3,8,1024]{3,2,1,0:T(8,128)S(1)} %get-tuple-element.44), channel_id=1, source_target_pairs={{0,16},{2,18},{4,20},{6,22},{8,24},{10,26},{12,28},{14,30},{16,0},... | collective-permute-start | bytes 294920 | tf_op jit(solution)/shard_map/ppermute | solution.py:416
  86.5 2.5 %collective-permute-start.4 = (f32[1,3,8,1024]{3,2,1,0:T(8,128)S(1)}, f32[1,3,8,1024]{3,2,1,0:T(8,128)S(1)}, u32[]{:S(2)}, u32[]{:S(2)}) collective-permute-start(f32[1,3,8,1024]{3,2,1,0:T(8,128)S(1)} %get-tuple-element.45), channel_id=1, source_target_pairs={{0,8},{2,10},{4,12},{6,14},{8,0},{10,2},{12,4},{14,6},{16,24},{18,... | collective-permute-start | bytes 294920 | tf_op jit(solution)/shard_map/ppermute | solution.py:416
  89.0 0.4 collective-permute-start.5
  89.4 1.2 %collective-permute-done.12.rest_7_ = f32[1,1,8,1024]{3,2,1,0:T(8,128)S(1)} collective-permute-done((f32[1,1,8,1024]{3,2,1,0:T(8,128)S(1)}, f32[1,1,8,1024]{3,2,1,0:T(8,128)S(1)}, u32[]{:S(2)}, u32[]{:S(2)}) %collective-permute-start.12) | collective-permute-done | bytes 32800 | tf_op jit(solution)/shard_map/ppermute | solution.py:416
  90.7 4.9 %collective-permute-done.3.rest_1_ = f32[1,3,8,1024]{3,2,1,0:T(8,128)S(1)} collective-permute-done((f32[1,3,8,1024]{3,2,1,0:T(8,128)S(1)}, f32[1,3,8,1024]{3,2,1,0:T(8,128)S(1)}, u32[]{:S(2)}, u32[]{:S(2)}) %collective-permute-start.3) | collective-permute-done | bytes 98336 | tf_op jit(solution)/shard_map/ppermute | solution.py:416
  95.6 1.7 %shard_map.82 = f32[2,4,4,1024]{3,2,1,0:T(4,128)} custom-call(s32[4]{0:T(128)S(1)} %and_select_fusion.order_ref, s32[1,1024]{1,0:T(1,128)S(1)} %get-tuple-element.31.place_ref, f32[1,3,8,1024]{3,2,1,0:T(8,128)S(1)} %get-tuple-element.43.rest_0_, f32[1,3,8,1024]{3,2,1,0:T(8,128)S(1)} %collective-permute-done.3.rest_1_, ...), custom_call_target="tpu_custom_call" | custom-call | tf_op jit(solution)/shard_map/pallas_call | solution.py:647
  (29 shorter events, 0.2 us)
Async XLA Ops:
  0.0 5.5 %copy-start.1 = (f32[2,2,8,128,128]{4,3,2,1,0:T(8,128)S(1)}, f32[2,2,8,128,128]{4,3,2,1,0:T(8,128)}, u32[]{:S(2)}) copy-start(f32[2,2,8,128,128]{4,3,2,1,0:T(8,128)} %right_ref.1) | copy-start | bytes 6291460
  0.0 6.4 %copy-start.5 = (f32[2,128]{1,0:T(2,128)S(1)}, f32[2,128]{1,0:T(2,128)}, u32[]{:S(2)}) copy-start(f32[2,128]{1,0:T(2,128)} %constant.31.clone.table_ref) | copy-start | bytes 3076
  0.0 6.4 %copy-start.4 = (s32[16384]{0:T(1024)S(1)}, s32[16384]{0:T(1024)}, u32[]{:S(2)}) copy-start(s32[16384]{0:T(1024)} %param.9) | copy-start | bytes 196612
  2.5 27.3 %collective-permute-start = (f32[2,1,8,128,128]{4,3,2,1,0:T(8,128)}, f32[2,1,8,128,128]{4,3,2,1,0:T(8,128)}, u32[]{:S(2)}, u32[]{:S(2)}) collective-permute-start(f32[2,1,8,128,128]{4,3,2,1,0:T(8,128)} %slice.9), channel_id=1, source_target_pairs={{0,1},{1,0},{2,3},{3,2},{4,5},{5,4},{6,7},{7,6},{8,9},{9,8},{10,11... | collective-permute-start | bytes 3145736 | tf_op jit(solution)/shard_map/ppermute | solution.py:27
  6.4 38.5 %collective-permute-start.7 = (f32[2,1,4,128,128]{4,3,2,1,0:T(8,128)}, f32[2,1,4,128,128]{4,3,2,1,0:T(8,128)S(1)}, u32[]{:S(2)}, u32[]{:S(2)}) collective-permute-start(f32[2,1,4,128,128]{4,3,2,1,0:T(8,128)} %get-tuple-element.57), channel_id=1, source_target_pairs={{0,1},{1,0},{2,3},{3,2},{4,5},{5,4},{6,7},{7,6},{8,9},{9,8},{10,11... | collective-permute-start | bytes 1572872 | tf_op jit(solution)/shard_map/ppermute | solution.py:27
  6.4 4.4 %copy-start = (f32[2,4,8,128,128]{4,3,2,1,0:T(8,128)S(1)}, f32[2,4,8,128,128]{4,3,2,1,0:T(8,128)}, u32[]{:S(2)}) copy-start(f32[2,4,8,128,128]{4,3,2,1,0:T(8,128)} %left_ref.7) | copy-start | bytes 12582916
  6.4 4.4 %copy-start.2 = (bf16[256,768]{1,0:T(8,128)(2,1)S(1)}, bf16[256,768]{1,0:T(8,128)(2,1)}, u32[]{:S(2)}) copy-start(bf16[256,768]{1,0:T(8,128)(2,1)} %constant.32.clone.table_y_ref) | copy-start | bytes 1179652
  6.4 4.4 %copy-start.3 = (bf16[768,256]{1,0:T(8,128)(2,1)S(1)}, bf16[768,256]{1,0:T(8,128)(2,1)}, u32[]{:S(2)}) copy-start(bf16[768,256]{1,0:T(8,128)(2,1)} %constant.33.clone.table_x_ref) | copy-start | bytes 1179652
  42.7 22.8 %collective-permute-start.1 = (f32[8,3,8,1024]{3,2,1,0:T(8,128)S(1)}, f32[8,3,8,1024]{3,2,1,0:T(8,128)S(1)}, u32[]{:S(2)}, u32[]{:S(2)}) collective-permute-start(f32[8,3,8,1024]{3,2,1,0:T(8,128)S(1)} %get-tuple-element.40), channel_id=1, source_target_pairs={{0,2},{2,0},{4,6},{6,4},{8,10},{10,8},{12,14},{14,12},{16,18},{18,... | collective-permute-start | bytes 2359304 | tf_op jit(solution)/shard_map/ppermute | solution.py:416
  42.8 14.6 %collective-permute-start.6 = (f32[2,1,4,128,128]{4,3,2,1,0:T(8,128)S(1)}, f32[2,1,4,128,128]{4,3,2,1,0:T(8,128)S(1)}, u32[]{:S(2)}, u32[]{:S(2)}) collective-permute-start(f32[2,1,4,128,128]{4,3,2,1,0:T(8,128)S(1)} %get-tuple-element.58), channel_id=1, source_target_pairs={{0,1},{1,0},{2,3},{3,2},{4,5},{5,4},{6,7},{7,6},{8,9},{9,8},{10,11... | collective-permute-start | bytes 1572872 | tf_op jit(solution)/shard_map/ppermute | solution.py:27
  65.5 23.9 %copy-start.6 = (s32[4]{0:T(128)S(1)}, s32[4]{0:T(128)}, u32[]{:S(2)}) copy-start(s32[4]{0:T(128)} %param.10) | copy-start | bytes 52
  65.5 1.9 %collective-permute-start.8 = (f32[8,1,8,1024]{3,2,1,0:T(8,128)S(1)}, f32[8,1,8,1024]{3,2,1,0:T(8,128)S(1)}, u32[]{:S(2)}, u32[]{:S(2)}) collective-permute-start(f32[8,1,8,1024]{3,2,1,0:T(8,128)S(1)} %get-tuple-element.50), channel_id=1, source_target_pairs={{0,2},{2,0},{4,6},{6,4},{8,10},{10,8},{12,14},{14,12},{16,18},{18,... | collective-permute-start | bytes 786440 | tf_op jit(solution)/shard_map/ppermute | solution.py:416
  65.7 18.9 %collective-permute-start.2 = (f32[4,3,8,1024]{3,2,1,0:T(8,128)S(1)}, f32[4,3,8,1024]{3,2,1,0:T(8,128)S(1)}, u32[]{:S(2)}, u32[]{:S(2)}) collective-permute-start(f32[4,3,8,1024]{3,2,1,0:T(8,128)S(1)} %get-tuple-element.42), channel_id=1, source_target_pairs={{0,4},{2,6},{4,0},{6,2},{8,12},{10,14},{12,8},{14,10},{16,20},{18,... | collective-permute-start | bytes 1179656 | tf_op jit(solution)/shard_map/ppermute | solution.py:416
  67.5 12.6 %collective-permute-start.9 = (f32[4,1,8,1024]{3,2,1,0:T(8,128)S(1)}, f32[4,1,8,1024]{3,2,1,0:T(8,128)S(1)}, u32[]{:S(2)}, u32[]{:S(2)}) collective-permute-start(f32[4,1,8,1024]{3,2,1,0:T(8,128)S(1)} %get-tuple-element.52), channel_id=1, source_target_pairs={{0,4},{2,6},{4,0},{6,2},{8,12},{10,14},{12,8},{14,10},{16,20},{18,... | collective-permute-start | bytes 393224 | tf_op jit(solution)/shard_map/ppermute | solution.py:416
  80.0 9.0 %collective-permute-start.10 = (f32[1,1,8,1024]{3,2,1,0:T(8,128)S(1)}, f32[1,1,8,1024]{3,2,1,0:T(8,128)S(1)}, u32[]{:S(2)}, u32[]{:S(2)}) collective-permute-start(f32[1,1,8,1024]{3,2,1,0:T(8,128)S(1)} %get-tuple-element.54), channel_id=1, source_target_pairs={{0,16},{2,18},{4,20},{6,22},{8,24},{10,26},{12,28},{14,30},{16,0},... | collective-permute-start | bytes 98312 | tf_op jit(solution)/shard_map/ppermute | solution.py:416
  82.9 6.5 %collective-permute-start.11 = (f32[1,1,8,1024]{3,2,1,0:T(8,128)S(1)}, f32[1,1,8,1024]{3,2,1,0:T(8,128)S(1)}, u32[]{:S(2)}, u32[]{:S(2)}) collective-permute-start(f32[1,1,8,1024]{3,2,1,0:T(8,128)S(1)} %get-tuple-element.55), channel_id=1, source_target_pairs={{0,8},{2,10},{4,12},{6,14},{8,0},{10,2},{12,4},{14,6},{16,24},{18,... | collective-permute-start | bytes 98312 | tf_op jit(solution)/shard_map/ppermute | solution.py:416
  84.5 6.2 %collective-permute-start.12 = (f32[1,1,8,1024]{3,2,1,0:T(8,128)S(1)}, f32[1,1,8,1024]{3,2,1,0:T(8,128)S(1)}, u32[]{:S(2)}, u32[]{:S(2)}) collective-permute-start(f32[1,1,8,1024]{3,2,1,0:T(8,128)S(1)} %get-tuple-element.56), channel_id=1, source_target_pairs={{0,24},{2,26},{4,28},{6,30},{8,16},{10,18},{12,20},{14,22},{16,8},... | collective-permute-start | bytes 98312 | tf_op jit(solution)/shard_map/ppermute | solution.py:416
  84.6 11.1 %collective-permute-start.3 = (f32[1,3,8,1024]{3,2,1,0:T(8,128)S(1)}, f32[1,3,8,1024]{3,2,1,0:T(8,128)S(1)}, u32[]{:S(2)}, u32[]{:S(2)}) collective-permute-start(f32[1,3,8,1024]{3,2,1,0:T(8,128)S(1)} %get-tuple-element.44), channel_id=1, source_target_pairs={{0,16},{2,18},{4,20},{6,22},{8,24},{10,26},{12,28},{14,30},{16,0},... | collective-permute-start | bytes 294920 | tf_op jit(solution)/shard_map/ppermute | solution.py:416
  86.5 9.1 %collective-permute-start.4 = (f32[1,3,8,1024]{3,2,1,0:T(8,128)S(1)}, f32[1,3,8,1024]{3,2,1,0:T(8,128)S(1)}, u32[]{:S(2)}, u32[]{:S(2)}) collective-permute-start(f32[1,3,8,1024]{3,2,1,0:T(8,128)S(1)} %get-tuple-element.45), channel_id=1, source_target_pairs={{0,8},{2,10},{4,12},{6,14},{8,0},{10,2},{12,4},{14,6},{16,24},{18,... | collective-permute-start | bytes 294920 | tf_op jit(solution)/shard_map/ppermute | solution.py:416
  89.0 6.6 %collective-permute-start.5 = (f32[1,3,8,1024]{3,2,1,0:T(8,128)S(1)}, f32[1,3,8,1024]{3,2,1,0:T(8,128)S(1)}, u32[]{:S(2)}, u32[]{:S(2)}) collective-permute-start(f32[1,3,8,1024]{3,2,1,0:T(8,128)S(1)} %get-tuple-element.46), channel_id=1, source_target_pairs={{0,24},{2,26},{4,28},{6,30},{8,16},{10,18},{12,20},{14,22},{16,8},... | collective-permute-start | bytes 294920 | tf_op jit(solution)/shard_map/ppermute | solution.py:416

commit v3 on v2

--- a/solution.py
+++ b/solution.py
@@ -286,12 +286,15 @@
                     put_single(2 * a + 1, seconds)
             return 0
 
-        def two_couples(a, _):
-            couple(2 * a, 0)
-            return couple(2 * a + 1, 0)
-
-        if groups % 4 == 0 and pairs < SUB:
-            lax.fori_loop(0, groups // 4, two_couples, 0)
+        batch = 4 if tiles <= 2 else 2
+
+        def couples(a, _):
+            for k in range(batch):
+                couple(batch * a + k, 0)
+            return 0
+
+        if groups % (2 * batch) == 0 and pairs < SUB:
+            lax.fori_loop(0, groups // (2 * batch), couples, 0)
         else:
             lax.fori_loop(0, groups // 2, couple, 0)
 

time: 97.5 us -> 97.3 us (level)
  no operation moved by 1% of the time
where the time goes in v3:
time: 97.3 us; the launch traced here: 97.1 us
  Pallas kernels  50.9 us (52%)
  waiting for transfers between devices  25 us (26%)
  starting transfers between devices  17.7 us (18%)
  local copies, waits for them, and re-layouts  3.4 us (3%)
    pallas_call x4, Pallas kernels, chunk_sums(): pl.pallas_call(partial(chunk_kernel, plan), out_shape=[like, like] if is_...  44.7 us
    ppermute x10, waiting for transfers between devices, moved(): return lax.ppermute(value, axis, route)  17.3 us
    ppermute x10, starting transfers between devices, moved(): return lax.ppermute(value, axis, route)  12.6 us
    ppermute x3, waiting for transfers between devices, swapped(): return lax.ppermute(block, axis, route)  7.7 us
    ppermute x3, starting transfers between devices, swapped(): return lax.ppermute(block, axis, route)  5.09 us
    pallas_call x1, Pallas kernels, listed(): pl.pallas_call(partial(list_kernel, plan), out_shape=[jax.ShapeDtypeStruc...  4.33 us
    slice x2, local copies, waits for them, and re-layouts, local(): sent.append(swapped(right_bands[:, bands, low:high], 'band', 0))  3.37 us
  transfers between devices with their start and end apart: 13, of which 5 were waited for; matrix products, arithmetic and copies ran while one was open for 1% of the time, Pallas kernels for 51%

profile of v3, /device:TPU:0, one launch (start us, length us, event | category | flops | bytes accessed | tf_op | source)
XLA Modules:
  0.0 97.1 jit_solution(3385192137945694706)
XLA Ops:
  0.0 2.5 %slice.9 = f32[2,1,8,128,128]{4,3,2,1,0:T(8,128)} slice(f32[2,2,8,128,128]{4,3,2,1,0:T(8,128)} %right_ref.1), slice={[0:2], [0:1], [0:8], [0:128], [0:128]} | slice | bytes 2097152 | tf_op jit(solution)/shard_map/slice | solution.py:674
  2.5 3.0 %collective-permute-start = (f32[2,1,8,128,128]{4,3,2,1,0:T(8,128)}, f32[2,1,8,128,128]{4,3,2,1,0:T(8,128)}, u32[]{:S(2)}, u32[]{:S(2)}) collective-permute-start(f32[2,1,8,128,128]{4,3,2,1,0:T(8,128)} %slice.9), channel_id=1, source_target_pairs={{0,1},{1,0},{2,3},{3,2},{4,5},{5,4},{6,7},{7,6},{8,9},{9,8},{10,11... | collective-permute-start | bytes 3145736 | tf_op jit(solution)/shard_map/ppermute | solution.py:27
  5.5 0.9 fusion.1
  6.4 4.3 %shard_map.73 = (s32[1]{0:T(128)}, s32[1,1024]{1,0:T(1,128)S(1)}, s32[2,128,128]{2,1,0:T(8,128)S(1)}, s32[128,128]{1,0:T(8,128)S(1)}, f32[5,2,128,128]{3,2,1,0:T(8,128)S(1)}) custom-call(s32[1]{0:T(128)} %bitcast.me_ref, s32[128,128]{1,0:T(8,128)S(1)} %bitcast.2, f32[2,128]{1,0:T(2,128)S(1)} %copy-done.5), custom_call_target="tpu_custom_call" | custom-call | flops 10000000000 | bytes 1000000 | tf_op jit(solution)/shard_map/pallas_call | solution.py:593
  10.8 18.3 %shard_map.74 = (f32[8,2,8,1024]{3,2,1,0:T(8,128)S(1)}, f32[8,2,8,1024]{3,2,1,0:T(8,128)S(1)}) custom-call(s32[1]{0:T(128)} %get-tuple-element.32.near_ref, f32[2,4,8,128,128]{4,3,2,1,0:T(8,128)S(1)} %copy-done, f32[2,2,8,128,128]{4,3,2,1,0:T(8,128)S(1)} %copy-done.1, bf16[256,768]{1,0:T(8,128)(2,1)S(1)} %copy-done.2, bf16[768,256]{1,0:T(8,128)(2,1)S(1)} %copy-done.3, ...), custom_call_target="tpu_custom_call" | custom-call | flops 6442450944 | bytes 4194304 | tf_op jit(solution)/shard_map/pallas_call | solution.py:373
  29.1 0.7 collective-permute-done.right_ref
  29.8 12.9 %shard_map.75 = (f32[8,3,8,1024]{3,2,1,0:T(8,128)S(1)}, f32[8,3,8,1024]{3,2,1,0:T(8,128)S(1)}) custom-call(s32[1]{0:T(128)} %get-tuple-element.32.near_ref, f32[2,4,8,128,128]{4,3,2,1,0:T(8,128)S(1)} %copy-done, f32[2,1,8,128,128]{4,3,2,1,0:T(8,128)} %collective-permute-done.right_ref, bf16[256,768]{1,0:T(8,128)(2,1)S(1)} %copy-done.2, ...), custom_call_target="tpu_custom_call" | custom-call | flops 3221225472 | bytes 4194304 | tf_op jit(solution)/shard_map/pallas_call | solution.py:373
  42.8 2.1 %collective-permute-start.6 = (f32[2,1,4,128,128]{4,3,2,1,0:T(8,128)S(1)}, f32[2,1,4,128,128]{4,3,2,1,0:T(8,128)S(1)}, u32[]{:S(2)}, u32[]{:S(2)}) collective-permute-start(f32[2,1,4,128,128]{4,3,2,1,0:T(8,128)S(1)} %get-tuple-element.58), channel_id=1, source_target_pairs={{0,1},{1,0},{2,3},{3,2},{4,5},{5,4},{6,7},{7,6},{8,9},{9,8},{10,11... | collective-permute-start | bytes 1572872 | tf_op jit(solution)/shard_map/ppermute | solution.py:27
  44.9 5.5 %shard_map.78.rest_0_ = f32[128,1,8,128]{3,2,1,0:T(8,128)S(1)} custom-call(s32[1]{0:T(128)} %get-tuple-element.32.near_ref, f32[2,4,8,128,128]{4,3,2,1,0:T(8,128)S(1)} %copy-done, f32[2,1,4,128,128]{4,3,2,1,0:T(8,128)S(1)} %collective-permute-done.7.right_ref, bf16[256,768]{1,0:T(8,128)(2,1)S(1)} %copy-done.2, bf16[768,256]{1,0:T(8,128)(2,1)S(1)} %copy-done.3, ...), custom_call_target="tpu_custom_call" | custom-call | flops 1610612736 | bytes 4194304 | tf_op jit(solution)/shard_map/pallas_call | solution.py:373
  50.4 7.0 %collective-permute-done.6.right_ref = f32[2,1,4,128,128]{4,3,2,1,0:T(8,128)S(1)} collective-permute-done((f32[2,1,4,128,128]{4,3,2,1,0:T(8,128)S(1)}, f32[2,1,4,128,128]{4,3,2,1,0:T(8,128)S(1)}, u32[]{:S(2)}, u32[]{:S(2)}) %collective-permute-start.6) | collective-permute-done | bytes 524320 | tf_op jit(solution)/shard_map/ppermute | solution.py:27
  57.4 7.9 %shard_map.79 = (f32[8,1,8,1024]{3,2,1,0:T(8,128)S(1)}, f32[8,1,8,1024]{3,2,1,0:T(8,128)S(1)}) custom-call(s32[1]{0:T(128)} %get-tuple-element.32.near_ref, f32[2,4,8,128,128]{4,3,2,1,0:T(8,128)S(1)} %copy-done, f32[2,1,4,128,128]{4,3,2,1,0:T(8,128)S(1)} %collective-permute-done.6.right_ref, bf16[256,768]{1,0:T(8,128)(2,1)S(1)} %copy-done.2, ...), custom_call_target="tpu_custom_call" | custom-call | flops 1610612736 | bytes 4194304 | tf_op jit(solution)/shard_map/pallas_call | solution.py:373
  65.3 0.1 collective-permute-start.8
  65.4 0.1 shard_map.76
  65.5 1.8 %collective-permute-start.2 = (f32[4,3,8,1024]{3,2,1,0:T(8,128)S(1)}, f32[4,3,8,1024]{3,2,1,0:T(8,128)S(1)}, u32[]{:S(2)}, u32[]{:S(2)}) collective-permute-start(f32[4,3,8,1024]{3,2,1,0:T(8,128)S(1)} %get-tuple-element.42), channel_id=1, source_target_pairs={{0,4},{2,6},{4,0},{6,2},{8,12},{10,14},{12,8},{14,10},{16,20},{18,... | collective-permute-start | bytes 1179656 | tf_op jit(solution)/shard_map/ppermute | solution.py:419
  67.3 1.4 %collective-permute-start.9 = (f32[4,1,8,1024]{3,2,1,0:T(8,128)S(1)}, f32[4,1,8,1024]{3,2,1,0:T(8,128)S(1)}, u32[]{:S(2)}, u32[]{:S(2)}) collective-permute-start(f32[4,1,8,1024]{3,2,1,0:T(8,128)S(1)} %get-tuple-element.52), channel_id=1, source_target_pairs={{0,4},{2,6},{4,0},{6,2},{8,12},{10,14},{12,8},{14,10},{16,20},{18,... | collective-permute-start | bytes 393224 | tf_op jit(solution)/shard_map/ppermute | solution.py:419
  68.7 11.1 %collective-permute-done.9.got_ref = f32[4,1,8,1024]{3,2,1,0:T(8,128)S(1)} collective-permute-done((f32[4,1,8,1024]{3,2,1,0:T(8,128)S(1)}, f32[4,1,8,1024]{3,2,1,0:T(8,128)S(1)}, u32[]{:S(2)}, u32[]{:S(2)}) %collective-permute-start.9) | collective-permute-done | bytes 131104 | tf_op jit(solution)/shard_map/ppermute | solution.py:419
  79.9 2.9 %collective-permute-start.10 = (f32[1,1,8,1024]{3,2,1,0:T(8,128)S(1)}, f32[1,1,8,1024]{3,2,1,0:T(8,128)S(1)}, u32[]{:S(2)}, u32[]{:S(2)}) collective-permute-start(f32[1,1,8,1024]{3,2,1,0:T(8,128)S(1)} %get-tuple-element.54), channel_id=1, source_target_pairs={{0,16},{2,18},{4,20},{6,22},{8,24},{10,26},{12,28},{14,30},{16,0},... | collective-permute-start | bytes 98312 | tf_op jit(solution)/shard_map/ppermute | solution.py:419
  82.8 1.6 %collective-permute-start.11 = (f32[1,1,8,1024]{3,2,1,0:T(8,128)S(1)}, f32[1,1,8,1024]{3,2,1,0:T(8,128)S(1)}, u32[]{:S(2)}, u32[]{:S(2)}) collective-permute-start(f32[1,1,8,1024]{3,2,1,0:T(8,128)S(1)} %get-tuple-element.55), channel_id=1, source_target_pairs={{0,8},{2,10},{4,12},{6,14},{8,0},{10,2},{12,4},{14,6},{16,24},{18,... | collective-permute-start | bytes 98312 | tf_op jit(solution)/shard_map/ppermute | solution.py:419
  84.4 2.0 %collective-permute-start.3 = (f32[1,3,8,1024]{3,2,1,0:T(8,128)S(1)}, f32[1,3,8,1024]{3,2,1,0:T(8,128)S(1)}, u32[]{:S(2)}, u32[]{:S(2)}) collective-permute-start(f32[1,3,8,1024]{3,2,1,0:T(8,128)S(1)} %get-tuple-element.44), channel_id=1, source_target_pairs={{0,16},{2,18},{4,20},{6,22},{8,24},{10,26},{12,28},{14,30},{16,0},... | collective-permute-start | bytes 294920 | tf_op jit(solution)/shard_map/ppermute | solution.py:419
  86.4 2.5 %collective-permute-start.4 = (f32[1,3,8,1024]{3,2,1,0:T(8,128)S(1)}, f32[1,3,8,1024]{3,2,1,0:T(8,128)S(1)}, u32[]{:S(2)}, u32[]{:S(2)}) collective-permute-start(f32[1,3,8,1024]{3,2,1,0:T(8,128)S(1)} %get-tuple-element.45), channel_id=1, source_target_pairs={{0,8},{2,10},{4,12},{6,14},{8,0},{10,2},{12,4},{14,6},{16,24},{18,... | collective-permute-start | bytes 294920 | tf_op jit(solution)/shard_map/ppermute | solution.py:419
  88.8 0.4 collective-permute-start.5
  89.3 1.2 %collective-permute-done.12.rest_7_ = f32[1,1,8,1024]{3,2,1,0:T(8,128)S(1)} collective-permute-done((f32[1,1,8,1024]{3,2,1,0:T(8,128)S(1)}, f32[1,1,8,1024]{3,2,1,0:T(8,128)S(1)}, u32[]{:S(2)}, u32[]{:S(2)}) %collective-permute-start.12) | collective-permute-done | bytes 32800 | tf_op jit(solution)/shard_map/ppermute | solution.py:419
  90.5 4.9 %collective-permute-done.3.rest_1_ = f32[1,3,8,1024]{3,2,1,0:T(8,128)S(1)} collective-permute-done((f32[1,3,8,1024]{3,2,1,0:T(8,128)S(1)}, f32[1,3,8,1024]{3,2,1,0:T(8,128)S(1)}, u32[]{:S(2)}, u32[]{:S(2)}) %collective-permute-start.3) | collective-permute-done | bytes 98336 | tf_op jit(solution)/shard_map/ppermute | solution.py:419
  95.4 1.7 %shard_map.82 = f32[2,4,4,1024]{3,2,1,0:T(4,128)} custom-call(s32[4]{0:T(128)S(1)} %and_select_fusion.order_ref, s32[1,1024]{1,0:T(1,128)S(1)} %get-tuple-element.31.place_ref, f32[1,3,8,1024]{3,2,1,0:T(8,128)S(1)} %get-tuple-element.43.rest_0_, f32[1,3,8,1024]{3,2,1,0:T(8,128)S(1)} %collective-permute-done.3.rest_1_, ...), custom_call_target="tpu_custom_call" | custom-call | tf_op jit(solution)/shard_map/pallas_call | solution.py:650
  (29 shorter events, 0.2 us)
Async XLA Ops:
  0.0 5.5 %copy-start.1 = (f32[2,2,8,128,128]{4,3,2,1,0:T(8,128)S(1)}, f32[2,2,8,128,128]{4,3,2,1,0:T(8,128)}, u32[]{:S(2)}) copy-start(f32[2,2,8,128,128]{4,3,2,1,0:T(8,128)} %right_ref.1) | copy-start | bytes 6291460
  0.0 6.4 %copy-start.5 = (f32[2,128]{1,0:T(2,128)S(1)}, f32[2,128]{1,0:T(2,128)}, u32[]{:S(2)}) copy-start(f32[2,128]{1,0:T(2,128)} %constant.31.clone.table_ref) | copy-start | bytes 3076
  0.0 6.4 %copy-start.4 = (s32[16384]{0:T(1024)S(1)}, s32[16384]{0:T(1024)}, u32[]{:S(2)}) copy-start(s32[16384]{0:T(1024)} %param.9) | copy-start | bytes 196612
  2.5 27.3 %collective-permute-start = (f32[2,1,8,128,128]{4,3,2,1,0:T(8,128)}, f32[2,1,8,128,128]{4,3,2,1,0:T(8,128)}, u32[]{:S(2)}, u32[]{:S(2)}) collective-permute-start(f32[2,1,8,128,128]{4,3,2,1,0:T(8,128)} %slice.9), channel_id=1, source_target_pairs={{0,1},{1,0},{2,3},{3,2},{4,5},{5,4},{6,7},{7,6},{8,9},{9,8},{10,11... | collective-permute-start | bytes 3145736 | tf_op jit(solution)/shard_map/ppermute | solution.py:27
  6.4 38.5 %collective-permute-start.7 = (f32[2,1,4,128,128]{4,3,2,1,0:T(8,128)}, f32[2,1,4,128,128]{4,3,2,1,0:T(8,128)S(1)}, u32[]{:S(2)}, u32[]{:S(2)}) collective-permute-start(f32[2,1,4,128,128]{4,3,2,1,0:T(8,128)} %get-tuple-element.57), channel_id=1, source_target_pairs={{0,1},{1,0},{2,3},{3,2},{4,5},{5,4},{6,7},{7,6},{8,9},{9,8},{10,11... | collective-permute-start | bytes 1572872 | tf_op jit(solution)/shard_map/ppermute | solution.py:27
  6.4 4.4 %copy-start = (f32[2,4,8,128,128]{4,3,2,1,0:T(8,128)S(1)}, f32[2,4,8,128,128]{4,3,2,1,0:T(8,128)}, u32[]{:S(2)}) copy-start(f32[2,4,8,128,128]{4,3,2,1,0:T(8,128)} %left_ref.7) | copy-start | bytes 12582916
  6.4 4.4 %copy-start.2 = (bf16[256,768]{1,0:T(8,128)(2,1)S(1)}, bf16[256,768]{1,0:T(8,128)(2,1)}, u32[]{:S(2)}) copy-start(bf16[256,768]{1,0:T(8,128)(2,1)} %constant.32.clone.table_y_ref) | copy-start | bytes 1179652
  6.4 4.4 %copy-start.3 = (bf16[768,256]{1,0:T(8,128)(2,1)S(1)}, bf16[768,256]{1,0:T(8,128)(2,1)}, u32[]{:S(2)}) copy-start(bf16[768,256]{1,0:T(8,128)(2,1)} %constant.33.clone.table_x_ref) | copy-start | bytes 1179652
  42.7 22.7 %collective-permute-start.1 = (f32[8,3,8,1024]{3,2,1,0:T(8,128)S(1)}, f32[8,3,8,1024]{3,2,1,0:T(8,128)S(1)}, u32[]{:S(2)}, u32[]{:S(2)}) collective-permute-start(f32[8,3,8,1024]{3,2,1,0:T(8,128)S(1)} %get-tuple-element.40), channel_id=1, source_target_pairs={{0,2},{2,0},{4,6},{6,4},{8,10},{10,8},{12,14},{14,12},{16,18},{18,... | collective-permute-start | bytes 2359304 | tf_op jit(solution)/shard_map/ppermute | solution.py:419
  42.8 14.6 %collective-permute-start.6 = (f32[2,1,4,128,128]{4,3,2,1,0:T(8,128)S(1)}, f32[2,1,4,128,128]{4,3,2,1,0:T(8,128)S(1)}, u32[]{:S(2)}, u32[]{:S(2)}) collective-permute-start(f32[2,1,4,128,128]{4,3,2,1,0:T(8,128)S(1)} %get-tuple-element.58), channel_id=1, source_target_pairs={{0,1},{1,0},{2,3},{3,2},{4,5},{5,4},{6,7},{7,6},{8,9},{9,8},{10,11... | collective-permute-start | bytes 1572872 | tf_op jit(solution)/shard_map/ppermute | solution.py:27
  65.3 23.9 %copy-start.6 = (s32[4]{0:T(128)S(1)}, s32[4]{0:T(128)}, u32[]{:S(2)}) copy-start(s32[4]{0:T(128)} %param.10) | copy-start | bytes 52
  65.3 1.9 %collective-permute-start.8 = (f32[8,1,8,1024]{3,2,1,0:T(8,128)S(1)}, f32[8,1,8,1024]{3,2,1,0:T(8,128)S(1)}, u32[]{:S(2)}, u32[]{:S(2)}) collective-permute-start(f32[8,1,8,1024]{3,2,1,0:T(8,128)S(1)} %get-tuple-element.50), channel_id=1, source_target_pairs={{0,2},{2,0},{4,6},{6,4},{8,10},{10,8},{12,14},{14,12},{16,18},{18,... | collective-permute-start | bytes 786440 | tf_op jit(solution)/shard_map/ppermute | solution.py:419
  65.5 18.9 %collective-permute-start.2 = (f32[4,3,8,1024]{3,2,1,0:T(8,128)S(1)}, f32[4,3,8,1024]{3,2,1,0:T(8,128)S(1)}, u32[]{:S(2)}, u32[]{:S(2)}) collective-permute-start(f32[4,3,8,1024]{3,2,1,0:T(8,128)S(1)} %get-tuple-element.42), channel_id=1, source_target_pairs={{0,4},{2,6},{4,0},{6,2},{8,12},{10,14},{12,8},{14,10},{16,20},{18,... | collective-permute-start | bytes 1179656 | tf_op jit(solution)/shard_map/ppermute | solution.py:419
  67.3 12.6 %collective-permute-start.9 = (f32[4,1,8,1024]{3,2,1,0:T(8,128)S(1)}, f32[4,1,8,1024]{3,2,1,0:T(8,128)S(1)}, u32[]{:S(2)}, u32[]{:S(2)}) collective-permute-start(f32[4,1,8,1024]{3,2,1,0:T(8,128)S(1)} %get-tuple-element.52), channel_id=1, source_target_pairs={{0,4},{2,6},{4,0},{6,2},{8,12},{10,14},{12,8},{14,10},{16,20},{18,... | collective-permute-start | bytes 393224 | tf_op jit(solution)/shard_map/ppermute | solution.py:419
  79.9 9.0 %collective-permute-start.10 = (f32[1,1,8,1024]{3,2,1,0:T(8,128)S(1)}, f32[1,1,8,1024]{3,2,1,0:T(8,128)S(1)}, u32[]{:S(2)}, u32[]{:S(2)}) collective-permute-start(f32[1,1,8,1024]{3,2,1,0:T(8,128)S(1)} %get-tuple-element.54), channel_id=1, source_target_pairs={{0,16},{2,18},{4,20},{6,22},{8,24},{10,26},{12,28},{14,30},{16,0},... | collective-permute-start | bytes 98312 | tf_op jit(solution)/shard_map/ppermute | solution.py:419
  82.8 6.5 %collective-permute-start.11 = (f32[1,1,8,1024]{3,2,1,0:T(8,128)S(1)}, f32[1,1,8,1024]{3,2,1,0:T(8,128)S(1)}, u32[]{:S(2)}, u32[]{:S(2)}) collective-permute-start(f32[1,1,8,1024]{3,2,1,0:T(8,128)S(1)} %get-tuple-element.55), channel_id=1, source_target_pairs={{0,8},{2,10},{4,12},{6,14},{8,0},{10,2},{12,4},{14,6},{16,24},{18,... | collective-permute-start | bytes 98312 | tf_op jit(solution)/shard_map/ppermute | solution.py:419
  84.3 6.2 %collective-permute-start.12 = (f32[1,1,8,1024]{3,2,1,0:T(8,128)S(1)}, f32[1,1,8,1024]{3,2,1,0:T(8,128)S(1)}, u32[]{:S(2)}, u32[]{:S(2)}) collective-permute-start(f32[1,1,8,1024]{3,2,1,0:T(8,128)S(1)} %get-tuple-element.56), channel_id=1, source_target_pairs={{0,24},{2,26},{4,28},{6,30},{8,16},{10,18},{12,20},{14,22},{16,8},... | collective-permute-start | bytes 98312 | tf_op jit(solution)/shard_map/ppermute | solution.py:419
  84.4 11.1 %collective-permute-start.3 = (f32[1,3,8,1024]{3,2,1,0:T(8,128)S(1)}, f32[1,3,8,1024]{3,2,1,0:T(8,128)S(1)}, u32[]{:S(2)}, u32[]{:S(2)}) collective-permute-start(f32[1,3,8,1024]{3,2,1,0:T(8,128)S(1)} %get-tuple-element.44), channel_id=1, source_target_pairs={{0,16},{2,18},{4,20},{6,22},{8,24},{10,26},{12,28},{14,30},{16,0},... | collective-permute-start | bytes 294920 | tf_op jit(solution)/shard_map/ppermute | solution.py:419
  86.4 9.1 %collective-permute-start.4 = (f32[1,3,8,1024]{3,2,1,0:T(8,128)S(1)}, f32[1,3,8,1024]{3,2,1,0:T(8,128)S(1)}, u32[]{:S(2)}, u32[]{:S(2)}) collective-permute-start(f32[1,3,8,1024]{3,2,1,0:T(8,128)S(1)} %get-tuple-element.45), channel_id=1, source_target_pairs={{0,8},{2,10},{4,12},{6,14},{8,0},{10,2},{12,4},{14,6},{16,24},{18,... | collective-permute-start | bytes 294920 | tf_op jit(solution)/shard_map/ppermute | solution.py:419
  88.8 6.6 %collective-permute-start.5 = (f32[1,3,8,1024]{3,2,1,0:T(8,128)S(1)}, f32[1,3,8,1024]{3,2,1,0:T(8,128)S(1)}, u32[]{:S(2)}, u32[]{:S(2)}) collective-permute-start(f32[1,3,8,1024]{3,2,1,0:T(8,128)S(1)} %get-tuple-element.46), channel_id=1, source_target_pairs={{0,24},{2,26},{4,28},{6,30},{8,16},{10,18},{12,20},{14,22},{16,8},... | collective-permute-start | bytes 294920 | tf_op jit(solution)/shard_map/ppermute | solution.py:419
